TPU v7x, 128 devices: a whole 4x4x4 slice. The times are simulated.
128 devices in a mesh: atom: 32 (over y, z, core), aux: 4 (over x).
Axes of the slice: x: 4, y: 4, z: 4, core: 2. Of those that a mesh axis runs over, the one named last changes fastest.
Arguments:
- pao_blocks: bfloat16 [64, 24, 15360], P('atom', None, 'aux'), may hold values from -0.048339844 to 0.048339844
- cabs_blocks: bfloat16 [64, 48, 15360], P('atom', None, 'aux'), may hold values from -0.3046875 to 0.3046875
- cabs_weight: bfloat16 [64, 48], P('atom'), may hold values from 0.25 to 4
- pair_blocks: int32 [2048, 4], P('atom'), may hold values from 0 to 63, as said below
- pao_size: int32 [2048], P('atom'), may hold values from 24 to 96
- cabs_size: int32 [2048], P('atom'), may hold values from 48 to 192
Outputs:
- v_pairs: float32 [2048, 96, 96], P('atom', 'aux')
Inputs may be any that keep to these rules, and one draw needn't show every extreme that they name: `pair_blocks`: each row names 4 different atom blocks; atom block b belongs to owner b // 2, and the 64 rows of one index of atom name at most one block of each owner.
All inputs are finite; a program needn't handle non-finite values.
Results may differ from a plain program's by a relative error of at most 0.0003.
Values may be sent and summed in bfloat16 or wider, within the bound.
A program may use at most 128 MiB of HBM per device.

v0:
```python
import jax
import jax.numpy as jnp
from jax import lax
from jax.sharding import PartitionSpec as P


def sent_together(arrays, axis, dim, along):
    ends, at = ([], 0)
    for a in arrays[:-1]:
        at += a.shape[along]
        ends.append(at)
    both = jnp.concatenate(arrays, axis=along)
    return tuple(
        jnp.split(lax.psum_scatter(both, axis, scatter_dimension=dim, tiled=True), ends, axis=along)
    )


def collect(pieces):
    return (pieces[0], pieces[1], pieces[2])


def shards(pao_blocks, cabs_blocks, cabs_weight, pair_blocks, pao_size, cabs_size):
    owners = lax.axis_size("atom")
    blk_dev = pao_blocks.shape[0]
    pao_rows = pao_blocks.shape[1]
    cabs_rows = cabs_blocks.shape[1]
    aux_local = pao_blocks.shape[2]
    pair_count = pair_blocks.shape[0]
    dom_count = pair_blocks.shape[1]
    pao_width = dom_count * pao_rows
    cabs_width = dom_count * cabs_rows
    flat_blocks = pair_blocks.reshape(-1)
    owner_ids = flat_blocks // blk_dev
    owner_range = jnp.arange(owners, dtype=jnp.int32)
    matches = owner_ids[:, None] == owner_range[None, :]
    wanted = jnp.max(jnp.where(matches, flat_blocks[:, None], -1), axis=0)
    every_pao, every_cabs, every_weight = collect(
        (
            lax.all_gather(pao_blocks, "atom", axis=0, tiled=True),
            lax.all_gather(cabs_blocks, "atom", axis=0, tiled=True),
            lax.all_gather(cabs_weight, "atom", axis=0, tiled=True),
        )
    )
    chosen = jnp.maximum(wanted, 0)
    slot_pao = jnp.take(every_pao, chosen, axis=0)
    slot_cabs = jnp.take(every_cabs, chosen, axis=0)
    slot_weight = jnp.take(every_weight, chosen, axis=0)
    slot_of = owner_ids.reshape(pair_count, dom_count)
    group_size = 4
    groups = slot_of.reshape(pair_count // group_size, group_size, dom_count)

    def pair_products(slots):
        rows_pao = jnp.take(slot_pao, slots.reshape(-1), axis=0).reshape(
            group_size, pao_width, aux_local
        )
        rows_cabs = jnp.take(slot_cabs, slots.reshape(-1), axis=0).reshape(
            group_size, cabs_width, aux_local
        )
        margin_part = jnp.einsum(
            "pia,pja->pij", rows_pao, rows_pao, preferred_element_type=jnp.float32
        )
        coupling_part = jnp.einsum(
            "pia,pja->pij", rows_pao, rows_cabs, preferred_element_type=jnp.float32
        )
        return (margin_part, coupling_part)

    margin, coupling = lax.map(pair_products, groups)
    margin = margin.reshape(pair_count, pao_width, pao_width)
    coupling = coupling.reshape(pair_count, pao_width, cabs_width)
    keep_pao = (jnp.arange(pao_width, dtype=jnp.int32)[None, :] < pao_size[:, None]).astype(
        jnp.float32
    )
    keep_cabs = (jnp.arange(cabs_width, dtype=jnp.int32)[None, :] < cabs_size[:, None]).astype(
        jnp.float32
    )
    margin = margin * keep_pao[:, :, None] * keep_pao[:, None, :]
    coupling = coupling * keep_pao[:, :, None] * keep_cabs[:, None, :]
    scales = (
        jnp.take(slot_weight, slot_of.reshape(-1), axis=0)
        .reshape(pair_count, cabs_width)
        .astype(jnp.float32)
    )
    margin_rows, coupling_rows = sent_together((margin, coupling), "aux", 1, 2)
    coupling_full = lax.all_gather(coupling_rows, "aux", axis=1, tiled=True)
    return margin_rows - jnp.einsum(
        "pix,pjx->pij",
        coupling_rows * scales[:, None, :],
        coupling_full,
        precision=lax.Precision.HIGHEST,
    )


def solution(mesh):
    placed = (
        P("atom", None, "aux"),
        P("atom", None, "aux"),
        P("atom", None),
        P("atom", None),
        P("atom"),
        P("atom"),
    )
    return jax.shard_map(
        shards, mesh=mesh, in_specs=placed, out_specs=P("atom", "aux", None), check_vma=False
    )
```

profile of v0, /device:TPU:1, one launch (start us, length us, event | category | flops | bytes accessed | tf_op | source)
XLA Modules:
  0.0 739.9 jit_solution(4457633753350145893)
XLA Ops:
  10.6 63.6 %all-gather.5.cloned.1.call-done = bf16[64,24,3840]{2,1,0:T(8,128)(2,1)} async-done(((bf16[2,24,3840]{2,1,0:T(8,128)(2,1)}), bf16[64,24,3840]{2,1,0:T(8,128)(2,1)}) %all-gather.5.cloned.1.call-update) | async-done | bytes 11796496 | tf_op jit(solution)/shard_map/all_gather | solution.py:39
  74.3 7.9 %gather_fusion.2 = bf16[32,24,3840]{2,1,0:T(8,128)(2,1)} fusion(bf16[64,24,3840]{2,1,0:T(8,128)(2,1)} %all-gather.5.cloned.1.call-done, s32[1024]{0:T(1024)S(1)} %pad_clamp_fusion.2), kind=kCustom, calls=%fused_computation.2 | custom fusion | bytes 11796608 | tf_op jit(solution)/shard_map/jit(_take)/gather | solution.py:45
  88.0 76.2 %all-gather.7.cloned.1.call-done = bf16[64,48,3840]{2,1,0:T(8,128)(2,1)} async-done(((bf16[2,48,3840]{2,1,0:T(8,128)(2,1)}), bf16[64,48,3840]{2,1,0:T(8,128)(2,1)}) %all-gather.7.cloned.1.call-update) | async-done | bytes 23592976 | tf_op jit(solution)/shard_map/all_gather | solution.py:40
  164.2 14.0 %gather_fusion.3 = bf16[32,48,3840]{2,1,0:T(8,128)(2,1)} fusion(bf16[64,48,3840]{2,1,0:T(8,128)(2,1)} %all-gather.7.cloned.1.call-done, s32[1024]{0:T(1024)S(1)} %pad_clamp_fusion.2), kind=kCustom, calls=%fused_computation.3 | custom fusion | bytes 23593088 | tf_op jit(solution)/shard_map/jit(_take)/gather | solution.py:46
  178.2 10.3 %broadcast_select_fusion = bf16[32,48,3840]{2,1,0:T(8,128)(2,1)} fusion(bf16[32,48,3840]{2,1,0:T(8,128)(2,1)} %gather_fusion.3, pred[32]{0:T(512)(128)(4,1)S(1)} %broadcast_compare_fusion), kind=kLoop, calls=%fused_computation.18 | loop fusion | flops 5898240 | bytes 23592992 | tf_op jit(solution)/shard_map/jit(_take)/select_n | solution.py:46
  188.5 368.7 %while.12 = (s32[]{:T(128)}, f32[16,4,96,96]{3,2,1,0:T(8,128)}, f32[16,4,96,192]{3,2,1,0:T(8,128)}, s32[16,4,4]{2,1,0:T(4,128)S(1)}, bf16[32,24,3840]{2,1,0:T(8,...) while((s32[]{:T(128)}, f32[16,4,96,96]{3,2,1,0:T(8,128)}, f32[16,4,96,192]{3,2,1,0:T(8,128)}, ...), condition=%wide.region_2.3_spmd, body=%wide.region_1.2_spmd.sunk | while | flops 853771392 | bytes 50735296 | solution.py:67
  195.9 7.8 %gather_fusion.1 = bf16[16,48,3840]{2,1,0:T(8,128)(2,1)} fusion(bf16[32,48,3840]{2,1,0:T(8,128)(2,1)} %get-tuple-element.114, s32[1024]{0:T(1024)S(1)} %pad_clamp_fusion.4), kind=kCustom, calls=%fused_computation.1.clone.1 | custom fusion | bytes 11796544 | tf_op jit(solution)/shard_map/while/body/eval_jaxpr/jit(_take)/gather | solution.py:56
  219.0 7.8 %gather_fusion.1 = bf16[16,48,3840]{2,1,0:T(8,128)(2,1)} fusion(bf16[32,48,3840]{2,1,0:T(8,128)(2,1)} %get-tuple-element.114, s32[1024]{0:T(1024)S(1)} %pad_clamp_fusion.4), kind=kCustom, calls=%fused_computation.1.clone.1 | custom fusion | bytes 11796544 | tf_op jit(solution)/shard_map/while/body/eval_jaxpr/jit(_take)/gather | solution.py:56
  242.1 7.8 %gather_fusion.1 = bf16[16,48,3840]{2,1,0:T(8,128)(2,1)} fusion(bf16[32,48,3840]{2,1,0:T(8,128)(2,1)} %get-tuple-element.114, s32[1024]{0:T(1024)S(1)} %pad_clamp_fusion.4), kind=kCustom, calls=%fused_computation.1.clone.1 | custom fusion | bytes 11796544 | tf_op jit(solution)/shard_map/while/body/eval_jaxpr/jit(_take)/gather | solution.py:56
  265.1 7.8 %gather_fusion.1 = bf16[16,48,3840]{2,1,0:T(8,128)(2,1)} fusion(bf16[32,48,3840]{2,1,0:T(8,128)(2,1)} %get-tuple-element.114, s32[1024]{0:T(1024)S(1)} %pad_clamp_fusion.4), kind=kCustom, calls=%fused_computation.1.clone.1 | custom fusion | bytes 11796544 | tf_op jit(solution)/shard_map/while/body/eval_jaxpr/jit(_take)/gather | solution.py:56
  288.1 7.8 %gather_fusion.1 = bf16[16,48,3840]{2,1,0:T(8,128)(2,1)} fusion(bf16[32,48,3840]{2,1,0:T(8,128)(2,1)} %get-tuple-element.114, s32[1024]{0:T(1024)S(1)} %pad_clamp_fusion.4), kind=kCustom, calls=%fused_computation.1.clone.1 | custom fusion | bytes 11796544 | tf_op jit(solution)/shard_map/while/body/eval_jaxpr/jit(_take)/gather | solution.py:56
  311.2 7.8 %gather_fusion.1 = bf16[16,48,3840]{2,1,0:T(8,128)(2,1)} fusion(bf16[32,48,3840]{2,1,0:T(8,128)(2,1)} %get-tuple-element.114, s32[1024]{0:T(1024)S(1)} %pad_clamp_fusion.4), kind=kCustom, calls=%fused_computation.1.clone.1 | custom fusion | bytes 11796544 | tf_op jit(solution)/shard_map/while/body/eval_jaxpr/jit(_take)/gather | solution.py:56
  334.2 7.8 %gather_fusion.1 = bf16[16,48,3840]{2,1,0:T(8,128)(2,1)} fusion(bf16[32,48,3840]{2,1,0:T(8,128)(2,1)} %get-tuple-element.114, s32[1024]{0:T(1024)S(1)} %pad_clamp_fusion.4), kind=kCustom, calls=%fused_computation.1.clone.1 | custom fusion | bytes 11796544 | tf_op jit(solution)/shard_map/while/body/eval_jaxpr/jit(_take)/gather | solution.py:56
  357.3 7.8 %gather_fusion.1 = bf16[16,48,3840]{2,1,0:T(8,128)(2,1)} fusion(bf16[32,48,3840]{2,1,0:T(8,128)(2,1)} %get-tuple-element.114, s32[1024]{0:T(1024)S(1)} %pad_clamp_fusion.4), kind=kCustom, calls=%fused_computation.1.clone.1 | custom fusion | bytes 11796544 | tf_op jit(solution)/shard_map/while/body/eval_jaxpr/jit(_take)/gather | solution.py:56
  380.3 7.8 %gather_fusion.1 = bf16[16,48,3840]{2,1,0:T(8,128)(2,1)} fusion(bf16[32,48,3840]{2,1,0:T(8,128)(2,1)} %get-tuple-element.114, s32[1024]{0:T(1024)S(1)} %pad_clamp_fusion.4), kind=kCustom, calls=%fused_computation.1.clone.1 | custom fusion | bytes 11796544 | tf_op jit(solution)/shard_map/while/body/eval_jaxpr/jit(_take)/gather | solution.py:56
  403.4 7.8 %gather_fusion.1 = bf16[16,48,3840]{2,1,0:T(8,128)(2,1)} fusion(bf16[32,48,3840]{2,1,0:T(8,128)(2,1)} %get-tuple-element.114, s32[1024]{0:T(1024)S(1)} %pad_clamp_fusion.4), kind=kCustom, calls=%fused_computation.1.clone.1 | custom fusion | bytes 11796544 | tf_op jit(solution)/shard_map/while/body/eval_jaxpr/jit(_take)/gather | solution.py:56
  426.4 7.8 %gather_fusion.1 = bf16[16,48,3840]{2,1,0:T(8,128)(2,1)} fusion(bf16[32,48,3840]{2,1,0:T(8,128)(2,1)} %get-tuple-element.114, s32[1024]{0:T(1024)S(1)} %pad_clamp_fusion.4), kind=kCustom, calls=%fused_computation.1.clone.1 | custom fusion | bytes 11796544 | tf_op jit(solution)/shard_map/while/body/eval_jaxpr/jit(_take)/gather | solution.py:56
  449.4 7.8 %gather_fusion.1 = bf16[16,48,3840]{2,1,0:T(8,128)(2,1)} fusion(bf16[32,48,3840]{2,1,0:T(8,128)(2,1)} %get-tuple-element.114, s32[1024]{0:T(1024)S(1)} %pad_clamp_fusion.4), kind=kCustom, calls=%fused_computation.1.clone.1 | custom fusion | bytes 11796544 | tf_op jit(solution)/shard_map/while/body/eval_jaxpr/jit(_take)/gather | solution.py:56
  472.5 7.8 %gather_fusion.1 = bf16[16,48,3840]{2,1,0:T(8,128)(2,1)} fusion(bf16[32,48,3840]{2,1,0:T(8,128)(2,1)} %get-tuple-element.114, s32[1024]{0:T(1024)S(1)} %pad_clamp_fusion.4), kind=kCustom, calls=%fused_computation.1.clone.1 | custom fusion | bytes 11796544 | tf_op jit(solution)/shard_map/while/body/eval_jaxpr/jit(_take)/gather | solution.py:56
  495.5 7.8 %gather_fusion.1 = bf16[16,48,3840]{2,1,0:T(8,128)(2,1)} fusion(bf16[32,48,3840]{2,1,0:T(8,128)(2,1)} %get-tuple-element.114, s32[1024]{0:T(1024)S(1)} %pad_clamp_fusion.4), kind=kCustom, calls=%fused_computation.1.clone.1 | custom fusion | bytes 11796544 | tf_op jit(solution)/shard_map/while/body/eval_jaxpr/jit(_take)/gather | solution.py:56
  568.6 87.9 %reduce-scatter.2.cloned.1.call-done = f32[64,24,288]{2,1,0:T(8,128)} async-done(((f32[64,96,288]{2,1,0:T(8,128)}), f32[64,24,288]{2,1,0:T(8,128)}) %reduce-scatter.2.cloned.1.call-update) | async-done | bytes 1769488 | tf_op jit(solution)/shard_map/reduce_scatter | solution.py:14
  660.0 22.5 %all-gather = bf16[32,2,48]{2,1,0:T(2,128)(2,1)S(1)} all-gather(bf16[1,2,48]{2,1,0:T(2,128)(2,1)S(1)} %bitcast.64), channel_id=1, replica_groups=mesh['atom'=32,'aux'=4] {'atom'}, dimensions={0}, use_global_device_ids=true | all-gather | bytes 6336 | tf_op jit(solution)/shard_map/all_gather | solution.py:41
  684.3 41.0 %all-gather.9.cloned.1.call-done = f32[64,96,192]{2,1,0:T(8,128)} async-done(((f32[64,24,192]{2,1,0:T(8,128)}), f32[64,96,192]{2,1,0:T(8,128)}) %all-gather.9.cloned.1.call-update) | async-done | bytes 4718608 | tf_op jit(solution)/shard_map/all_gather | solution.py:84
  725.3 8.0 %fusion.7 = f32[64,24,96]{2,1,0:T(8,128)} fusion(f32[64,96,192]{2,1,0:T(8,128)} %all-gather.9.cloned.1.call-done, f32[64,24,288]{2,1,0:T(8,128)S(1)} %copy-done.1, f32[64,192]{1,0:T(8,128)S(1)} %select_convert_fusion), kind=kOutput, calls=%fused_computation.27 | convolution fusion | flops 340180992 | bytes 7127040 | tf_op jit(solution)/shard_map/pix,pjx->pij/dot_general | solution.py:85
  (254 shorter events, 285.5 us)
Async XLA Ops:
  6.5 67.7 %all-gather.5.cloned.1.call-start = ((), (), s32[]{:S(2)}) async-start(), calls=%async_computation.1 | async-start | bytes 12165120 | tf_op jit(solution)/shard_map/all_gather | solution.py:39
  7.3 157.0 %all-gather.7.cloned.1.call-start = ((), (), s32[]{:S(2)}) async-start(), calls=%async_computation.2 | async-start | bytes 24330240 | tf_op jit(solution)/shard_map/all_gather | solution.py:40
  8.0 648.4 %reduce-scatter.2.cloned.1.call-start = ((), (), s32[]{:S(2)}) async-start(), calls=%async_computation.3 | async-start | bytes 11796480 | tf_op jit(solution)/shard_map/reduce_scatter | solution.py:14
  557.2 3.7 copy-start
  568.5 91.5 %copy-start.3 = (bf16[2,48]{1,0:T(2,128)(2,1)S(1)}, bf16[2,48]{1,0:T(2,128)(2,1)}, u32[]{:S(2)}) copy-start(bf16[2,48]{1,0:T(2,128)(2,1)} %param.10) | copy-start | bytes 580
  568.5 115.7 %copy-start.2 = (s32[64,4]{0,1:T(4,128)S(1)}, s32[64,4]{0,1:T(4,128)}, u32[]{:S(2)}) copy-start(s32[64,4]{0,1:T(4,128)} %param.11) | copy-start | bytes 3076
  568.5 156.8 %all-gather.9.cloned.1.call-start = ((), (), s32[]{:S(2)}) async-start(), calls=%async_computation.4 | async-start | bytes 7864320 | tf_op jit(solution)/shard_map/all_gather | solution.py:84
  656.4 68.9 %copy-start.1 = (f32[64,24,288]{2,1,0:T(8,128)S(1)}, f32[64,24,288]{2,1,0:T(8,128)}, u32[]{:S(2)}) copy-start(f32[64,24,288]{2,1,0:T(8,128)} %reduce-scatter.2.cloned.1.call-done) | copy-start | bytes 5308420
Sparse Core Ops, SparseCore 0:
  9.6 64.6 all-gather.4
  76.5 87.6 all-gather.6
  568.6 87.7 reduce-scatter.1
  660.0 65.2 all-gather.8
where the time goes:
time: 743 us; the launch traced here: 740 us
  waiting for transfers between devices  270 us (36%)
  local copies, waits for them, and re-layouts  241 us (32%)
  other arithmetic  115 us (15%)
  matrix products  77.5 us (10%)
  blocking collectives  22.5 us (3%)
  between operations  13.3 us (2%)
    gather x16, local copies, waits for them, and re-layouts, pair_products(): jnp.take(slot_cabs, slots.reshape(-1), axis=0)  125 us
    reduce_scatter x1, waiting for transfers between devices, sent_together(): lax.psum_scatter(both, axis, scatter_dimension=dim, tiled=True)  87.9 us
    gather x16, local copies, waits for them, and re-layouts, pair_products(): jnp.take(slot_pao, slots.reshape(-1), axis=0)  80.2 us
    all_gather x1, waiting for transfers between devices, shards(): lax.all_gather(cabs_blocks, 'atom', axis=0, tiled=True)  76.2 us
    all_gather x1, waiting for transfers between devices, shards(): lax.all_gather(pao_blocks, 'atom', axis=0, tiled=True)  63.6 us
    select_n x16, other arithmetic, pair_products(): jnp.take(slot_cabs, slots.reshape(-1), axis=0)  52.2 us
    dot_general x16, matrix products, pair_products(): jnp.einsum('pia,pja->pij', rows_pao, rows_cabs, preferred_element_type=jn...  43.9 us
    all_gather x1, waiting for transfers between devices, shards(): coupling_full = lax.all_gather(coupling_rows, 'aux', axis=1, tiled=True)  41 us
  transfers between devices with their start and end apart: 4, of which 4 were waited for; matrix products, arithmetic and copies ran while one was open for 2% of the time, Pallas kernels for 0%

commit v1 on v0

v1 whole, which is shorter than its diff:
```python
import jax
import jax.numpy as jnp
from jax import lax
from jax.experimental import pallas as pl
from jax.experimental.pallas import tpu as pltpu
from jax.sharding import PartitionSpec as P

TILES = 54


def pair_kernel(blk, gram, scale, out):
    x = lax.axis_index("aux")
    lane = lax.broadcasted_iota(jnp.int32, (8, 128), 1)

    def one_pair(p):
        picks = [blk[p * 4 + l] for l in range(4)]
        acc = None
        for l in range(4):
            off = picks[l] * 24
            lt = off // 128
            rem = off - lt * 128
            nxt = jnp.minimum(lt + 1, 11)
            lm = lt - 3 * x
            mine = jnp.logical_and(lm >= 0, lm < 3)
            lm0 = jnp.clip(lm, 0, 2)
            lm1 = jnp.clip(lm + 1, 0, 2)
            first, second = [], []
            for k in range(4):
                base = (picks[k] // 2) * TILES
                par = picks[k] % 2
                for t in range(3):
                    row = base + (par * 3 + t) * 3
                    first.append(gram[row + lm0])
                    second.append(gram[row + lm1])
            for k in range(4):
                base = (picks[k] // 2) * TILES + 18
                par = picks[k] % 2
                for ct in (par, 2):
                    first.append(gram[base + ct * 12 + lt])
                    second.append(gram[base + ct * 12 + nxt])
            a = jnp.concatenate(first, axis=0)
            b = jnp.concatenate(second, axis=0)
            lanes = lax.broadcasted_iota(jnp.int32, a.shape, 1)
            rows = lax.broadcasted_iota(jnp.int32, a.shape, 0)
            both = jnp.where(lanes >= rem, a, b)
            keep = jnp.logical_or(rows >= 96, mine)
            both = jnp.where(keep, both, 0.0)
            turned = pltpu.roll(both, lax.rem(24 * l - rem + 128, 128), 1)
            if acc is None:
                acc = jnp.where(lanes < 24, turned, 0.0)
            else:
                here = jnp.logical_and(lanes >= 24 * l, lanes < 24 * l + 24)
                acc = jnp.where(here, turned, acc)
        margin, c = acc[:96], acc[96:]
        cs = c * scale[p]
        c_hi = c.astype(jnp.bfloat16)
        c_lo = (c - c_hi.astype(jnp.float32)).astype(jnp.bfloat16)
        s_hi = cs.astype(jnp.bfloat16)
        s_lo = (cs - s_hi.astype(jnp.float32)).astype(jnp.bfloat16)
        left = jnp.concatenate([s_hi, s_lo, s_hi], axis=0)
        right = jnp.concatenate([c_hi, c_hi, c_lo], axis=0)
        prod = lax.dot_general(
            left, right, (((0,), (0,)), ((), ())), preferred_element_type=jnp.float32
        )
        return margin - prod[:96]

    @pl.loop(0, 16)
    def _(g):
        v = [one_pair(g * 4 + q) for q in range(4)]
        lanes = lax.broadcasted_iota(jnp.int32, (96, 128), 1)
        r1 = pltpu.roll(v[1], 96, 1)
        r2 = pltpu.roll(v[2], 64, 1)
        r3 = pltpu.roll(v[3], 32, 1)
        out[g, :, 0:128] = jnp.where(lanes < 96, v[0], r1)
        out[g, :, 128:256] = jnp.where(lanes < 64, r1, r2)
        out[g, :, 256:384] = jnp.where(lanes < 32, r2, r3)


def pair_parts(blk, gram, scale):
    return pl.pallas_call(
        pair_kernel,
        out_shape=jax.ShapeDtypeStruct((16, 96, 384), jnp.float32),
        in_specs=[
            pl.BlockSpec(memory_space=pltpu.SMEM),
            pl.BlockSpec(memory_space=pltpu.VMEM),
            pl.BlockSpec(memory_space=pltpu.VMEM),
        ],
        out_specs=pl.BlockSpec(memory_space=pltpu.VMEM),
        compiler_params=pltpu.CompilerParams(vmem_limit_bytes=60 * 1024 * 1024),
    )(blk, gram, scale)


def by_class(rows):
    parts = rows.reshape(2, 4, 12, rows.shape[-1])
    head = parts[:, :, :8].transpose(1, 0, 2, 3).reshape(4, 16, -1)
    tail = parts[:, :, 8:].transpose(1, 0, 2, 3).reshape(4, 8, -1)
    return jnp.concatenate([head, tail], axis=1).reshape(96, -1)


def tiled(a):
    r, c = a.shape
    return a.reshape(r // 8, 8, c // 128, 128).transpose(0, 2, 1, 3).reshape(-1, 8, 128)


def shards(pao_blocks, cabs_blocks, cabs_weight, pair_blocks, pao_size, cabs_size):
    x = lax.axis_index("aux")
    every = lax.all_gather(pao_blocks.reshape(48, -1), "atom", axis=0, tiled=True)
    own = jnp.concatenate([pao_blocks.reshape(48, -1), by_class(cabs_blocks)], axis=0)
    gram = lax.dot_general(
        own, every, (((1,), (1,)), ((), ())), preferred_element_type=jnp.float32
    )
    margin = lax.psum_scatter(gram[:48], "aux", scatter_dimension=1, tiled=True)
    coupling = lax.psum_scatter(gram[48:], "aux", scatter_dimension=0, tiled=True)
    held = jnp.concatenate([tiled(margin), tiled(coupling)], axis=0)
    grams = lax.all_gather(held, "atom", axis=0, tiled=True)

    weights = lax.all_gather(cabs_weight, "atom", axis=0, tiled=True)
    mine = lax.dynamic_slice_in_dim(weights, 12 * x, 12, axis=1).astype(jnp.float32)
    picked = jnp.take(mine, pair_blocks.reshape(-1), axis=0).reshape(64, 4, 12)
    at = (
        48 * jnp.arange(4, dtype=jnp.int32)[None, :, None]
        + 12 * x
        + jnp.arange(12, dtype=jnp.int32)[None, None, :]
    )
    picked = jnp.where(at < cabs_size[:, None, None], picked, 0.0)
    odd = (pair_blocks % 2 == 1)[:, :, None]
    tail = picked[:, :, 8:]
    zero = jnp.zeros_like(tail)
    scale = jnp.concatenate(
        [picked[:, :, :8], jnp.where(odd, zero, tail), jnp.where(odd, tail, zero)], axis=2
    ).reshape(64, 64)
    scale = jnp.broadcast_to(scale[:, :, None], (64, 64, 128))

    parts = pair_parts(pair_blocks.reshape(-1), grams, scale)
    rows = lax.psum_scatter(parts, "aux", scatter_dimension=1, tiled=True)
    rows = rows.reshape(16, 24, 4, 96).transpose(0, 2, 1, 3).reshape(64, 24, 96)
    size = pao_size[:, None, None]
    keep_row = (24 * x + jnp.arange(24, dtype=jnp.int32))[None, :, None] < size
    keep_col = jnp.arange(96, dtype=jnp.int32)[None, None, :] < size
    return jnp.where(jnp.logical_and(keep_row, keep_col), rows, 0.0)


def solution(mesh):
    placed = (
        P("atom", None, "aux"),
        P("atom", None, "aux"),
        P("atom", None),
        P("atom", None),
        P("atom"),
        P("atom"),
    )
    return jax.shard_map(
        shards, mesh=mesh, in_specs=placed, out_specs=P("atom", "aux", None), check_vma=False
    )
```

time: 743 us -> 243 us (0.33)
  local copies, waits for them, and re-layouts: 241 us -> 9.85 us
  other arithmetic: 115 us -> 3.38 us
  waiting for transfers between devices: 270 us -> 163 us
  matrix products: 77.5 us -> 8.28 us
  Pallas kernels: 0 us -> 20.9 us
    gather x37 -> x2, local copies, waits for them, and re-layouts: 229 us -> 0.83 us  [shards(): picked = jnp.take(mine, pair_blocks.reshape(-1), axis=0).reshape(64, 4, 12)]
    select_n x54 -> x4, other arithmetic: 103 us -> 1.24 us  [the longest x1 1.16 us: shards(): return jnp.where(jnp.logical_and(keep_row, keep_col), rows, 0.0)]
    all_gather x3 -> x2, waiting for transfers between devices: 181 us -> 91.2 us  [the longest x1 64.5 us: shards(): lax.all_gather(pao_blocks.reshape(48, -1), 'atom', axis=0, tiled=True)]
    dot_general x33 -> x1, matrix products: 77.5 us -> 8.28 us  [shards(): lax.dot_general(own, every, (((1,), (1,)), ((), ())), preferred_element_t...]
    pallas_call x0 -> x1, Pallas kernels: none -> 20.9 us  [pair_parts(): pl.pallas_call(pair_kernel, out_shape=jax.ShapeDtypeStruct((16, 96, 384),...]
    reduce_scatter x1 -> x3, waiting for transfers between devices: 87.9 us -> 70.8 us  [the longest x1 29.6 us: shards(): rows = lax.psum_scatter(parts, 'aux', scatter_dimension=1, tiled=True)]
  transfers between devices with their start and end apart: 4 -> 5, of which waited for: 4 -> 5; matrix products, arithmetic and copies ran while one was open for 2% -> 2% of each run, Pallas kernels for 0% -> 0%
where the time goes in v1:
time: 243 us
  waiting for transfers between devices  163 us (67%)
  blocking collectives  24.2 us (10%)
  Pallas kernels  20.9 us (9%)
  between operations  13.3 us (5%)
  local copies, waits for them, and re-layouts  9.85 us (4%)
  matrix products  8.28 us (3%)
  other arithmetic  3.38 us (1%)
    all_gather x1, waiting for transfers between devices, shards(): lax.all_gather(pao_blocks.reshape(48, -1), 'atom', axis=0, tiled=True)  64.5 us
    reduce_scatter x1, waiting for transfers between devices, shards(): rows = lax.psum_scatter(parts, 'aux', scatter_dimension=1, tiled=True)  29.6 us
    all_gather x1, waiting for transfers between devices, shards(): grams = lax.all_gather(held, 'atom', axis=0, tiled=True)  26.7 us
    reduce_scatter x1, waiting for transfers between devices, shards(): lax.psum_scatter(gram[48:], 'aux', scatter_dimension=0, tiled=True)  24.4 us
    all_gather x1, blocking collectives, shards(): weights = lax.all_gather(cabs_weight, 'atom', axis=0, tiled=True)  24.2 us
    pallas_call x1, Pallas kernels, pair_parts(): pl.pallas_call(pair_kernel, out_shape=jax.ShapeDtypeStruct((16, 96, 384),...  20.9 us
    reduce_scatter x1, waiting for transfers between devices, shards(): margin = lax.psum_scatter(gram[:48], 'aux', scatter_dimension=1, tiled=True)  16.8 us
    dot_general x1, matrix products, shards(): lax.dot_general(own, every, (((1,), (1,)), ((), ())), preferred_element_t...  8.28 us
  transfers between devices with their start and end apart: 5, of which 5 were waited for; matrix products, arithmetic and copies ran while one was open for 2% of the time, Pallas kernels for 0%

profile of v1, /device:TPU:1, one launch (start us, length us, event | category | flops | bytes accessed | tf_op | source)
XLA Modules:
  0.0 242.8 jit_solution(2952922726748090795)
XLA Ops:
  6.5 0.7 all-gather.4.cloned.1.call-update
  7.3 1.7 copy.18
  9.0 0.2 slice_bitcast_fusion.1
  9.2 0.1 copy.20
  9.3 0.3 slice_bitcast_fusion
  9.8 64.5 %all-gather.4.cloned.1.call-done = bf16[1536,3840]{1,0:T(8,128)(2,1)} async-done(((bf16[48,3840]{1,0:T(8,128)(2,1)}), bf16[1536,3840]{1,0:T(8,128)(2,1)}) %all-gather.4.cloned.1.call-update) | async-done | bytes 11796496 | tf_op jit(solution)/shard_map/all_gather | solution.py:107
  74.3 8.3 %fusion = f32[144,1536]{1,0:T(8,128)S(1)} fusion(bf16[1536,3840]{1,0:T(8,128)(2,1)} %all-gather.4.cloned.1.call-done, bf16[96,3840]{1,0:T(8,128)(2,1)S(1)} %bitcast.29, bf16[48,3840]{1,0:T(8,128)(2,1)S(1)} %bitcast.34), kind=kOutput, calls=%fused_computation.1 | convolution fusion | flops 1700904960 | bytes 13787136 | tf_op jit(solution)/shard_map/dot_general | solution.py:109
  82.6 0.7 slice.44
  83.4 0.9 slice.45
  84.3 16.8 %reduce-scatter.4.cloned.1.call-done = f32[48,384]{1,0:T(8,128)} async-done(((f32[48,1536]{1,0:T(8,128)}), f32[48,384]{1,0:T(8,128)}) %reduce-scatter.4.cloned.1.call-update) | async-done | bytes 73744 | tf_op jit(solution)/shard_map/reduce_scatter | solution.py:112
  101.1 24.4 %reduce-scatter.6.cloned.1.call-done = f32[24,1536]{1,0:T(8,128)} async-done(((f32[96,1536]{1,0:T(8,128)}), f32[24,1536]{1,0:T(8,128)}) %reduce-scatter.6.cloned.1.call-update) | async-done | bytes 147472 | tf_op jit(solution)/shard_map/reduce_scatter | solution.py:113
  125.5 1.7 pad_maximum_fusion.2
  127.3 0.7 reshape.168.blk
  128.0 0.1 reshape.178
  128.2 24.2 %all-gather = bf16[32,2,48]{2,1,0:T(2,128)(2,1)S(1)} all-gather(bf16[1,2,48]{2,1,0:T(2,128)(2,1)S(1)} %bitcast.42), channel_id=1, replica_groups=mesh['atom'=32,'aux'=4] {'atom'}, dimensions={0}, use_global_device_ids=true | all-gather | bytes 6336 | tf_op jit(solution)/shard_map/all_gather | solution.py:117
  152.4 0.7 gather_fusion
  153.2 0.1 copy.23
  153.6 26.7 %all-gather.6.cloned.1.call-done.gram = f32[1728,8,128]{2,1,0:T(8,128)} async-done(((f32[54,8,128]{2,1,0:T(8,128)}), f32[1728,8,128]{2,1,0:T(8,128)}) %all-gather.6.cloned.1.call-update) | async-done | bytes 7077904 | tf_op jit(solution)/shard_map/all_gather | solution.py:115
  180.3 1.9 broadcast_in_dim.52.scale
  182.2 20.9 %shard_map.64 = f32[16,96,384]{2,1,0:T(8,128)} custom-call(s32[256]{0:T(256)} %reshape.168.blk, f32[1728,8,128]{2,1,0:T(8,128)} %all-gather.6.cloned.1.call-done.gram, f32[64,64,128]{2,1,0:T(8,128)} %broadcast_in_dim.52.scale), custom_call_target="tpu_custom_call" | custom-call | tf_op jit(solution)/shard_map/pallas_call | solution.py:80
  203.1 0.6 copy-done.2
  203.9 29.6 %reduce-scatter.8.cloned.1.call-done = f32[16,24,384]{2,1,0:T(8,128)} async-done(((f32[16,96,384]{2,1,0:T(8,128)}), f32[16,24,384]{2,1,0:T(8,128)}) %reduce-scatter.8.cloned.1.call-update) | async-done | bytes 589840 | tf_op jit(solution)/shard_map/reduce_scatter | solution.py:135
  233.5 1.5 fusion.7
  235.1 1.2 and_select_fusion
  (37 shorter events, 1.1 us)
Async XLA Ops:
  6.5 67.7 %all-gather.4.cloned.1.call-start = ((), (), s32[]{:S(2)}) async-start(), calls=%async_computation.3 | async-start | bytes 12165120 | tf_op jit(solution)/shard_map/all_gather | solution.py:107
  7.3 93.8 %reduce-scatter.4.cloned.1.call-start = ((), (), s32[]{:S(2)}) async-start(), calls=%async_computation.4 | async-start | bytes 368640 | tf_op jit(solution)/shard_map/reduce_scatter | solution.py:112
  9.2 65.1 %copy-start = (bf16[2,24,3840]{2,1,0:T(8,128)(2,1)S(1)}, bf16[2,24,3840]{2,1,0:T(8,128)(2,1)}, u32[]{:S(2)}) copy-start(bf16[2,24,3840]{2,1,0:T(8,128)(2,1)} %param.6) | copy-start | bytes 1105924
  82.5 44.7 %copy-start.1 = (s32[64,4]{0,1:T(4,128)S(1)}, s32[64,4]{0,1:T(4,128)}, u32[]{:S(2)}) copy-start(s32[64,4]{0,1:T(4,128)} %param.9) | copy-start | bytes 3076
  82.6 45.6 %copy-start.4 = (bf16[2,48]{1,0:T(2,128)(2,1)S(1)}, bf16[2,48]{1,0:T(2,128)(2,1)}, u32[]{:S(2)}) copy-start(bf16[2,48]{1,0:T(2,128)(2,1)} %param.8) | copy-start | bytes 580
  83.3 70.1 %copy-start.3 = (s32[64]{0:T(128)S(1)}, s32[64]{0:T(128)}, u32[]{:S(2)}) copy-start(s32[64]{0:T(128)} %param.11) | copy-start | bytes 772
  83.3 42.2 %reduce-scatter.6.cloned.1.call-start = ((), (), s32[]{:S(2)}) async-start(), calls=%async_computation.5 | async-start | bytes 737280 | tf_op jit(solution)/shard_map/reduce_scatter | solution.py:113
  84.3 96.0 %all-gather.6.cloned.1.call-start = ((), (), s32[]{:S(2)}) async-start(), calls=%async_computation.6 | async-start | bytes 7299072 | tf_op jit(solution)/shard_map/all_gather | solution.py:115
  127.2 106.3 %reduce-scatter.8.cloned.1.call-start = ((), (), s32[]{:S(2)}) async-start(), calls=%async_computation.7 | async-start | bytes 2949120 | tf_op jit(solution)/shard_map/reduce_scatter | solution.py:135
  203.1 0.7 copy-start.2
Sparse Core Ops, SparseCore 0:
  9.6 64.6 all-gather.3
  83.4 17.6 reduce-scatter.3
  103.5 21.9 reduce-scatter.5
  127.6 52.6 all-gather.5
  203.2 30.2 reduce-scatter.7

commit v2 on v1

--- a/solution.py
+++ b/solution.py
@@ -1,3 +1,5 @@
+import functools
+
 import jax
 import jax.numpy as jnp
 from jax import lax
@@ -5,7 +7,267 @@
 from jax.experimental.pallas import tpu as pltpu
 from jax.sharding import PartitionSpec as P
 
+MESH = pl.DeviceIdType.MESH
+
 TILES = 54
+HELD = 55
+
+
+class Place:
+    def __init__(self):
+        self.me = lax.axis_index("atom")
+        self.x = lax.axis_index("aux")
+        self.core = lax.rem(self.me, 2)
+        self.z = lax.rem(self.me // 2, 4)
+        self.y = self.me // 8
+
+    def atom(self, y=0, z=0, flip=False):
+        core = 1 - self.core if flip else self.core
+        return (lax.rem(self.y + y + 4, 4) * 4 + lax.rem(self.z + z + 4, 4)) * 2 + core
+
+    def along(self, axis, step):
+        at = self.atom(**{axis: step})
+        return (at, self.x)
+
+    def partner(self):
+        return (self.atom(flip=True), self.x)
+
+    def beside(self, step):
+        return (self.me, lax.rem(self.x + step + 4, 4))
+
+
+def greet(devices):
+    barrier = pltpu.get_barrier_semaphore()
+    for device in devices:
+        pl.semaphore_signal(barrier, inc=1, device_id=device, device_id_type=MESH)
+    pl.semaphore_wait(barrier, len(devices))
+
+
+class Wires:
+    def __init__(self, send_sem, recv_sem):
+        self.send_sem, self.recv_sem, self.sent = send_sem, recv_sem, []
+
+    def copy(self, src, dst, at, device):
+        return pltpu.make_async_remote_copy(
+            src_ref=src,
+            dst_ref=dst,
+            send_sem=self.send_sem.at[at],
+            recv_sem=self.recv_sem.at[at],
+            device_id=device,
+            device_id_type=MESH,
+        )
+
+    def send(self, src, dst, at, device):
+        copy = self.copy(src, dst, at, device)
+        copy.start()
+        self.sent.append(copy)
+
+    def wait(self, view, at, device):
+        self.copy(view, view, at, device).wait_recv()
+
+    def drain(self):
+        for copy in self.sent:
+            copy.wait_send()
+        self.sent = []
+
+
+OFFSETS = (0, -1, 1, 2)
+PER_HALF = 36
+
+
+def gather_plane(place, wires, own, full, sub):
+    axes = (("z", "y"), ("y", "z"))
+
+    def origin(h, k, m, flip=False):
+        first, second = axes[h]
+        return place.atom(flip=flip, **{first: OFFSETS[k], second: OFFSETS[m]})
+
+    def one(h, k, m):
+        return full(h, origin(h, k, m))
+
+    def to(h, order, step):
+        return place.along(axes[h][order], step)
+
+    def base(h):
+        return h * PER_HALF
+
+    def across(h, k, m):
+        src = own(h) if (k, m) == (0, 0) else one(h, k, m)
+        wires.send(src, one(h, k, m), base(h) + 20 + 4 * k + m, place.partner())
+
+    def spread(h, k):
+        src = own(h) if k == 0 else one(h, k, 0)
+        dst = one(h, k, 0)
+        wires.send(src, dst, base(h) + 4 + 4 * k, to(h, 1, 1))
+        wires.send(src, dst, base(h) + 5 + 4 * k, to(h, 1, -1))
+
+    halves = (0, 1)
+    for h in halves:
+        wires.send(own(h), one(h, 0, 0), base(h), to(h, 0, 1))
+        wires.send(own(h), one(h, 0, 0), base(h) + 1, to(h, 0, -1))
+    for h in halves:
+        spread(h, 0)
+        across(h, 0, 0)
+    for h in halves:
+        for s, step in ((0, 1), (1, -1)):
+            k = s + 1
+            wires.wait(one(h, k, 0), base(h) + s, to(h, 0, step))
+            piece = sub(h, origin(h, k, 0), s)
+            wires.send(piece, piece, base(h) + 2 + s, to(h, 0, step))
+    for h in halves:
+        for k in (1, 2):
+            spread(h, k)
+            across(h, k, 0)
+
+    def forward(h, k):
+        for s, step in ((0, 1), (1, -1)):
+            m = s + 1
+            wires.wait(one(h, k, m), base(h) + 4 + 4 * k + s, to(h, 1, step))
+            piece = sub(h, origin(h, k, m), s)
+            wires.send(piece, piece, base(h) + 6 + 4 * k + s, to(h, 1, step))
+            across(h, k, m)
+
+    for h in halves:
+        forward(h, 0)
+    for h in halves:
+        for s, step in ((0, 1), (1, -1)):
+            wires.wait(sub(h, origin(h, 3, 0), s), base(h) + 2 + s, to(h, 0, step))
+        spread(h, 3)
+        across(h, 3, 0)
+    for k in (1, 2, 3):
+        for h in halves:
+            forward(h, k)
+    for k in range(4):
+        for h in halves:
+            for s, step in ((0, 1), (1, -1)):
+                wires.wait(
+                    sub(h, origin(h, k, 3), s), base(h) + 6 + 4 * k + s, to(h, 1, step)
+                )
+            across(h, k, 3)
+    for k in range(4):
+        for m in range(4):
+            for h in halves:
+                view = full(h, origin(h, k, m, flip=True))
+                wires.wait(view, base(h) + 20 + 4 * k + m, place.partner())
+
+
+def gram_kernel(
+    pao, own, weight, held, every, part, near, final,
+    send_a, recv_a, send_b, recv_b, send_c, recv_c, local,
+):
+    place = Place()
+    x = place.x
+    greet(
+        [place.along(a, s) for a in ("y", "z") for s in (1, -1)]
+        + [place.partner(), place.beside(1), place.beside(-1)]
+    )
+    keep = [
+        pltpu.make_async_copy(
+            pao.at[:, pl.ds(1920 * h, 1920)], every.at[h, place.me], local.at[h]
+        )
+        for h in range(2)
+    ]
+    for copy in keep:
+        copy.start()
+    wires = Wires(send_a, recv_a)
+    cuts = ((0, 1024), (1024, 896))
+    gather_plane(
+        place,
+        wires,
+        lambda h: pao.at[:, pl.ds(1920 * h, 1920)],
+        lambda h, atom: every.at[h, atom],
+        lambda h, atom, s: every.at[h, atom, :, pl.ds(*cuts[s])],
+    )
+    for copy in keep:
+        copy.wait()
+
+    nt = (((1,), (1,)), ((), ()))
+
+    @pl.loop(0, 4)
+    def _(line):
+        g = None
+        for h in range(2):
+            rows = every[h, pl.ds(line * 8, 8)].reshape(384, 1920)
+            d = lax.dot_general(
+                own[:, 1920 * h : 1920 * (h + 1)], rows, nt,
+                preferred_element_type=jnp.float32,
+            )
+            g = d if g is None else g + d
+        for r in range(6):
+            for c in range(3):
+                part[line, r * 3 + c] = g[8 * r : 8 * r + 8, 128 * c : 128 * c + 128]
+        for k in range(4):
+            for r in range(3):
+                for c in range(3):
+                    top = 48 + 24 * k + 8 * r
+                    part[k, 18 + r * 12 + line * 3 + c] = g[
+                        top : top + 8, 128 * c : 128 * c + 128
+                    ]
+
+    def klass(step):
+        return lax.rem(x + step + 4, 4)
+
+    ring = Wires(send_b, recv_b)
+    a, b = pl.ds(0, 27), pl.ds(27, 27)
+    left, right = place.beside(-1), place.beside(1)
+    ring.send(part.at[klass(2), a], near.at[0], 0, left)
+    ring.send(part.at[klass(2), b], near.at[1], 1, right)
+    ring.send(part.at[klass(-1), b], final.at[0, b], 2, left)
+    ring.send(part.at[klass(1), a], final.at[1, a], 3, right)
+    ring.wait(near.at[0], 0, left)
+    part[klass(-1), a] = part[klass(-1), a] + near[0]
+    ring.send(part.at[klass(-1), a], final.at[0, a], 4, left)
+    ring.wait(near.at[1], 1, right)
+    part[klass(1), b] = part[klass(1), b] + near[1]
+    ring.send(part.at[klass(1), b], final.at[1, b], 5, right)
+    ring.wait(final.at[0, b], 2, left)
+    ring.wait(final.at[1, a], 3, right)
+    ring.wait(final.at[0, a], 4, left)
+    ring.wait(final.at[1, b], 5, right)
+    held[place.me, pl.ds(0, TILES)] = part[x] + (final[0] + final[1])
+    held[place.me, TILES] = weight[...]
+
+    out = Wires(send_c, recv_c)
+    span = ((0, 28), (28, 27))
+    pieces = (((0, 14), (14, 14)), ((28, 14), (42, 13)))
+    gather_plane(
+        place,
+        out,
+        lambda h: held.at[place.me, pl.ds(*span[h])],
+        lambda h, atom: held.at[atom, pl.ds(*span[h])],
+        lambda h, atom, s: held.at[atom, pl.ds(*pieces[h][s])],
+    )
+    wires.drain()
+    ring.drain()
+    out.drain()
+
+
+def grams_of(pao, own, weight):
+    dma = pltpu.SemaphoreType.DMA
+    vmem = pl.BlockSpec(memory_space=pltpu.VMEM)
+    return pl.pallas_call(
+        gram_kernel,
+        out_shape=jax.ShapeDtypeStruct((32, HELD, 8, 128), jnp.float32),
+        in_specs=[vmem, vmem, vmem],
+        out_specs=vmem,
+        scratch_shapes=[
+            pltpu.VMEM((2, 32, 48, 1920), jnp.bfloat16),
+            pltpu.VMEM((4, TILES, 8, 128), jnp.float32),
+            pltpu.VMEM((2, 27, 8, 128), jnp.float32),
+            pltpu.VMEM((2, TILES, 8, 128), jnp.float32),
+            dma((2 * PER_HALF,)),
+            dma((2 * PER_HALF,)),
+            dma((6,)),
+            dma((6,)),
+            dma((2 * PER_HALF,)),
+            dma((2 * PER_HALF,)),
+            dma((2,)),
+        ],
+        compiler_params=pltpu.CompilerParams(
+            collective_id=0, has_side_effects=True, vmem_limit_bytes=48 * 1024 * 1024
+        ),
+        name="grams",
+    )(pao, own, weight)
 
 
 def pair_kernel(blk, gram, scale, out):
@@ -26,14 +288,14 @@
             lm1 = jnp.clip(lm + 1, 0, 2)
             first, second = [], []
             for k in range(4):
-                base = (picks[k] // 2) * TILES
+                base = (picks[k] // 2) * HELD
                 par = picks[k] % 2
                 for t in range(3):
                     row = base + (par * 3 + t) * 3
                     first.append(gram[row + lm0])
                     second.append(gram[row + lm1])
             for k in range(4):
-                base = (picks[k] // 2) * TILES + 18
+                base = (picks[k] // 2) * HELD + 18
                 par = picks[k] % 2
                 for ct in (par, 2):
                     first.append(gram[base + ct * 12 + lt])
@@ -97,25 +359,15 @@
     return jnp.concatenate([head, tail], axis=1).reshape(96, -1)
 
 
-def tiled(a):
-    r, c = a.shape
-    return a.reshape(r // 8, 8, c // 128, 128).transpose(0, 2, 1, 3).reshape(-1, 8, 128)
-
-
 def shards(pao_blocks, cabs_blocks, cabs_weight, pair_blocks, pao_size, cabs_size):
     x = lax.axis_index("aux")
-    every = lax.all_gather(pao_blocks.reshape(48, -1), "atom", axis=0, tiled=True)
-    own = jnp.concatenate([pao_blocks.reshape(48, -1), by_class(cabs_blocks)], axis=0)
-    gram = lax.dot_general(
-        own, every, (((1,), (1,)), ((), ())), preferred_element_type=jnp.float32
-    )
-    margin = lax.psum_scatter(gram[:48], "aux", scatter_dimension=1, tiled=True)
-    coupling = lax.psum_scatter(gram[48:], "aux", scatter_dimension=0, tiled=True)
-    held = jnp.concatenate([tiled(margin), tiled(coupling)], axis=0)
-    grams = lax.all_gather(held, "atom", axis=0, tiled=True)
-
-    weights = lax.all_gather(cabs_weight, "atom", axis=0, tiled=True)
-    mine = lax.dynamic_slice_in_dim(weights, 12 * x, 12, axis=1).astype(jnp.float32)
+    pao = pao_blocks.reshape(48, -1)
+    own = jnp.concatenate([pao, by_class(cabs_blocks)], axis=0)
+    weight = jnp.pad(cabs_weight.astype(jnp.float32), ((0, 6), (0, 80)))
+    held = grams_of(pao, own, weight)
+    grams = held.reshape(32 * HELD, 8, 128)
+    weights = held[:, TILES, :2, :48].reshape(64, 48)
+    mine = lax.dynamic_slice_in_dim(weights, 12 * x, 12, axis=1)
     picked = jnp.take(mine, pair_blocks.reshape(-1), axis=0).reshape(64, 4, 12)
     at = (
         48 * jnp.arange(4, dtype=jnp.int32)[None, :, None]

time: 243 us -> 158 us (0.65)
  waiting for transfers between devices: 163 us -> 27.8 us
  Pallas kernels: 20.9 us -> 104 us
  blocking collectives: 24.2 us -> 0 us
  matrix products: 8.28 us -> 0 us
    all_gather x2 -> x0, waiting for transfers between devices: 91.2 us -> none  [the longest x1 64.5 us: shards(): lax.all_gather(pao_blocks.reshape(48, -1), 'atom', axis=0, tiled=True)]
    pallas_call x0 -> x1, Pallas kernels: none -> 83.5 us  [grams_of(): pl.pallas_call(gram_kernel, out_shape=jax.ShapeDtypeStruct((32, HELD, 8,...]
    reduce_scatter x2 -> x0, waiting for transfers between devices: 41.2 us -> none  [the longest x1 24.4 us: shards(): lax.psum_scatter(gram[48:], 'aux', scatter_dimension=0, tiled=True)]
    all_gather x1 -> x0, blocking collectives: 24.2 us -> none  [shards(): weights = lax.all_gather(cabs_weight, 'atom', axis=0, tiled=True)]
    dot_general x1 -> x0, matrix products: 8.28 us -> none  [shards(): lax.dot_general(own, every, (((1,), (1,)), ((), ())), preferred_element_t...]
  transfers between devices with their start and end apart: 5 -> 1, of which waited for: 5 -> 1; matrix products, arithmetic and copies ran while one was open for 2% -> 0% of each run, Pallas kernels for 0% -> 0%
where the time goes in v2:
time: 158 us; the launch traced here: 157 us
  Pallas kernels  104 us (66%)
  waiting for transfers between devices  27.8 us (18%)
  between operations  13.6 us (9%)
  local copies, waits for them, and re-layouts  10 us (6%)
  other arithmetic  1.74 us (1%)
    pallas_call x1, Pallas kernels, grams_of(): pl.pallas_call(gram_kernel, out_shape=jax.ShapeDtypeStruct((32, HELD, 8,...  83.5 us
    reduce_scatter x1, waiting for transfers between devices, shards(): rows = lax.psum_scatter(parts, 'aux', scatter_dimension=1, tiled=True)  27.8 us
    pallas_call x1, Pallas kernels, pair_parts(): pl.pallas_call(pair_kernel, out_shape=jax.ShapeDtypeStruct((16, 96, 384),...  20.9 us
    unnamed x12, local copies, waits for them, and re-layouts  3.19 us
  transfers between devices with their start and end apart: 1, of which 1 were waited for; matrix products, arithmetic and copies ran while one was open for 0% of the time, Pallas kernels for 0%

profile of v2, /device:TPU:1, one launch (start us, length us, event | category | flops | bytes accessed | tf_op | source)
XLA Modules:
  0.0 157.5 jit_solution(17488004080247113948)
XLA Ops:
  6.5 1.7 %copy.17 = bf16[2,48,3840]{2,0,1:T(2,128)(2,1)S(1)} copy(bf16[2,48,3840]{2,1,0:T(8,128)(2,1)} %param.7) | data formatting | bytes 1474560 | tf_op args[1]
  8.2 0.3 slice_bitcast_fusion
  8.6 0.2 slice_bitcast_fusion.1
  8.8 0.1 copy.16
  8.9 0.1 reshape.165
  9.0 0.7 reshape.158.blk
  9.7 0.1 copy.19
  10.0 0.8 copy-done
  10.7 0.1 pad_maximum_fusion.own
  10.8 83.5 %grams.1 = f32[32,55,8,128]{3,2,1,0:T(8,128)} custom-call(bf16[48,3840]{1,0:T(8,128)(2,1)S(1)} %bitcast.18, bf16[144,3840]{1,0:T(8,128)(2,1)S(1)} %pad_maximum_fusion.own, f32[8,128]{1,0:T(8,128)S(1)} %pad_convert_fusion.weight), custom_call_target="tpu_custom_call" | custom-call | tf_op jit(solution)/shard_map/grams/pallas_call | solution.py:248
  94.3 0.9 slice.29
  95.3 0.1 constant_dynamic-slice_fusion
  95.3 0.7 gather_fusion
  96.1 0.1 copy.22
  96.2 0.1 select_select_fusion
  96.4 0.1 copy.23
  96.5 1.9 %broadcast_in_dim.52.scale = f32[64,64,128]{2,1,0:T(8,128)} broadcast(f32[64,64]{1,0:T(8,128)S(1)} %copy.23), dimensions={0,1} | broadcast | bytes 2113536 | tf_op jit(solution)/shard_map/broadcast_in_dim | solution.py:384
  98.4 20.9 %shard_map.64 = f32[16,96,384]{2,1,0:T(8,128)} custom-call(s32[256]{0:T(256)} %reshape.158.blk, f32[1760,8,128]{2,1,0:T(8,128)} %bitcast.19, f32[64,64,128]{2,1,0:T(8,128)} %broadcast_in_dim.52.scale), custom_call_target="tpu_custom_call" | custom-call | tf_op jit(solution)/shard_map/pallas_call | solution.py:342
  119.3 0.6 copy-done.2
  120.0 0.1 iota_compare_fusion
  120.1 27.8 %reduce-scatter.2.cloned.1.call-done = f32[16,24,384]{2,1,0:T(8,128)} async-done(((f32[16,96,384]{2,1,0:T(8,128)}), f32[16,24,384]{2,1,0:T(8,128)}) %reduce-scatter.2.cloned.1.call-update) | async-done | bytes 589840 | tf_op jit(solution)/shard_map/reduce_scatter | solution.py:387
  147.9 1.5 fusion.2
  149.4 0.1 pad_maximum_fusion.1
  149.5 1.2 and_select_fusion
  (24 shorter events, 0.4 us)
Async XLA Ops:
  6.5 141.3 %reduce-scatter.2.cloned.1.call-start = ((), (), s32[]{:S(2)}) async-start(), calls=%async_computation.1 | async-start | bytes 2949120 | tf_op jit(solution)/shard_map/reduce_scatter | solution.py:387
  6.5 2.2 %copy-start.1 = (s32[64,4]{0,1:T(4,128)S(1)}, s32[64,4]{0,1:T(4,128)}, u32[]{:S(2)}) copy-start(s32[64,4]{0,1:T(4,128)} %param.9) | copy-start | bytes 3076
  8.6 1.3 copy-start.4
  9.7 1.0 copy-start
  94.3 1.9 %copy-start.3 = (s32[64]{0:T(128)S(1)}, s32[64]{0:T(128)}, u32[]{:S(2)}) copy-start(s32[64]{0:T(128)} %param.11) | copy-start | bytes 772
  119.3 0.7 copy-start.2
Sparse Core Ops, SparseCore 0:
  119.5 28.3 reduce-scatter.1

commit v3 on v2

v3 whole, which is shorter than its diff:
```python
import jax
import jax.numpy as jnp
from jax import lax
from jax.experimental import pallas as pl
from jax.experimental.pallas import tpu as pltpu
from jax.sharding import PartitionSpec as P

MESH = pl.DeviceIdType.MESH

TILES = 54
HELD = 55


class Place:
    def __init__(self):
        self.me = lax.axis_index("atom")
        self.x = lax.axis_index("aux")
        self.core = lax.rem(self.me, 2)
        self.z = lax.rem(self.me // 2, 4)
        self.y = self.me // 8

    def atom(self, y=0, z=0, flip=False):
        core = 1 - self.core if flip else self.core
        return (lax.rem(self.y + y + 4, 4) * 4 + lax.rem(self.z + z + 4, 4)) * 2 + core

    def along(self, axis, step):
        at = self.atom(**{axis: step})
        return (at, self.x)

    def partner(self):
        return (self.atom(flip=True), self.x)

    def beside(self, step):
        return (self.me, lax.rem(self.x + step + 4, 4))


def greet(devices):
    barrier = pltpu.get_barrier_semaphore()
    for device in devices:
        pl.semaphore_signal(barrier, inc=1, device_id=device, device_id_type=MESH)
    pl.semaphore_wait(barrier, len(devices))


class Wires:
    def __init__(self, send_sem, recv_sem):
        self.send_sem, self.recv_sem, self.sent = send_sem, recv_sem, []

    def copy(self, src, dst, at, device):
        return pltpu.make_async_remote_copy(
            src_ref=src,
            dst_ref=dst,
            send_sem=self.send_sem.at[at],
            recv_sem=self.recv_sem.at[at],
            device_id=device,
            device_id_type=MESH,
        )

    def send(self, src, dst, at, device):
        copy = self.copy(src, dst, at, device)
        copy.start()
        self.sent.append(copy)

    def wait(self, view, at, device):
        self.copy(view, view, at, device).wait_recv()

    def drain(self):
        for copy in self.sent:
            copy.wait_send()
        self.sent = []


OFFSETS = (0, -1, 1, 2)
PER_HALF = 36


def gather_plane(place, wires, own, full, sub):
    axes = (("z", "y"), ("y", "z"))

    def origin(h, k, m, flip=False):
        first, second = axes[h]
        return place.atom(flip=flip, **{first: OFFSETS[k], second: OFFSETS[m]})

    def one(h, k, m):
        return full(h, origin(h, k, m))

    def to(h, order, step):
        return place.along(axes[h][order], step)

    def base(h):
        return h * PER_HALF

    def across(h, k, m):
        src = own(h) if (k, m) == (0, 0) else one(h, k, m)
        wires.send(src, one(h, k, m), base(h) + 20 + 4 * k + m, place.partner())

    def spread(h, k):
        src = own(h) if k == 0 else one(h, k, 0)
        dst = one(h, k, 0)
        wires.send(src, dst, base(h) + 4 + 4 * k, to(h, 1, 1))
        wires.send(src, dst, base(h) + 5 + 4 * k, to(h, 1, -1))

    halves = (0, 1)
    for h in halves:
        wires.send(own(h), one(h, 0, 0), base(h), to(h, 0, 1))
        wires.send(own(h), one(h, 0, 0), base(h) + 1, to(h, 0, -1))
    for h in halves:
        spread(h, 0)
        across(h, 0, 0)
    for h in halves:
        for s, step in ((0, 1), (1, -1)):
            k = s + 1
            wires.wait(one(h, k, 0), base(h) + s, to(h, 0, step))
            piece = sub(h, origin(h, k, 0), s)
            wires.send(piece, piece, base(h) + 2 + s, to(h, 0, step))
    for h in halves:
        for k in (1, 2):
            spread(h, k)
            across(h, k, 0)

    def forward(h, k):
        for s, step in ((0, 1), (1, -1)):
            m = s + 1
            wires.wait(one(h, k, m), base(h) + 4 + 4 * k + s, to(h, 1, step))
            piece = sub(h, origin(h, k, m), s)
            wires.send(piece, piece, base(h) + 6 + 4 * k + s, to(h, 1, step))
            across(h, k, m)

    for h in halves:
        forward(h, 0)
    for h in halves:
        for s, step in ((0, 1), (1, -1)):
            wires.wait(sub(h, origin(h, 3, 0), s), base(h) + 2 + s, to(h, 0, step))
        spread(h, 3)
        across(h, 3, 0)
    for k in (1, 2, 3):
        for h in halves:
            forward(h, k)
    for k in range(4):
        for h in halves:
            for s, step in ((0, 1), (1, -1)):
                wires.wait(
                    sub(h, origin(h, k, 3), s), base(h) + 6 + 4 * k + s, to(h, 1, step)
                )
            across(h, k, 3)
    for k in range(4):
        for m in range(4):
            for h in halves:
                view = full(h, origin(h, k, m, flip=True))
                wires.wait(view, base(h) + 20 + 4 * k + m, place.partner())


def kernel(
    blk, pao_size, cabs_size, pao, cabs, weight, out,
    own, every, part, near, final, held, vals, vnear, vfinal,
    send_a, recv_a, send_b, recv_b, send_c, recv_c, send_d, recv_d, local,
):
    place = Place()
    x = place.x
    load = [
        pltpu.make_async_copy(pao, own.at[pl.ds(0, 48)], local.at[0]),
        pltpu.make_async_copy(cabs, own.at[pl.ds(48, 96)], local.at[1]),
    ] + [
        pltpu.make_async_copy(
            pao.at[:, pl.ds(1920 * h, 1920)], every.at[h, place.me], local.at[2 + h]
        )
        for h in range(2)
    ]
    for copy in load:
        copy.start()
    greet(
        [place.along(a, s) for a in ("y", "z") for s in (1, -1)]
        + [place.partner(), place.beside(1), place.beside(-1)]
    )
    load[0].wait()
    wires = Wires(send_a, recv_a)
    cuts = ((0, 1024), (1024, 896))
    gather_plane(
        place,
        wires,
        lambda h: own.at[pl.ds(0, 48), pl.ds(1920 * h, 1920)],
        lambda h, atom: every.at[h, atom],
        lambda h, atom, s: every.at[h, atom, :, pl.ds(*cuts[s])],
    )
    for copy in load[1:]:
        copy.wait()

    nt = (((1,), (1,)), ((), ()))

    @pl.loop(0, 4)
    def _(line):
        g = None
        for h in range(2):
            rows = every[h, pl.ds(line * 8, 8)].reshape(384, 1920)
            d = lax.dot_general(
                own[:, 1920 * h : 1920 * (h + 1)], rows, nt,
                preferred_element_type=jnp.float32,
            )
            g = d if g is None else g + d
        for c in range(3):
            col = g[:, 128 * c : 128 * c + 128]
            for r in range(6):
                part[line, r * 3 + c] = col[8 * r : 8 * r + 8]
            for k in range(4):
                a, b = 48 + 12 * k, 96 + 12 * k
                at = 18 + line * 3 + c
                part[k, at] = col[a : a + 8]
                part[k, at + 12] = col[b : b + 8]
                part[k, at + 24] = jnp.concatenate(
                    [col[a + 8 : a + 12], col[b + 8 : b + 12]], axis=0
                )

    def klass(step):
        return lax.rem(x + step + 4, 4)

    ring = Wires(send_b, recv_b)
    a, b = pl.ds(0, 27), pl.ds(27, 27)
    left, right = place.beside(-1), place.beside(1)
    ring.send(part.at[klass(2), a], near.at[0], 0, left)
    ring.send(part.at[klass(2), b], near.at[1], 1, right)
    ring.send(part.at[klass(-1), b], final.at[0, b], 2, left)
    ring.send(part.at[klass(1), a], final.at[1, a], 3, right)
    ring.wait(near.at[0], 0, left)
    part[klass(-1), a] = part[klass(-1), a] + near[0]
    ring.send(part.at[klass(-1), a], final.at[0, a], 4, left)
    ring.wait(near.at[1], 1, right)
    part[klass(1), b] = part[klass(1), b] + near[1]
    ring.send(part.at[klass(1), b], final.at[1, b], 5, right)
    ring.wait(final.at[0, b], 2, left)
    ring.wait(final.at[1, a], 3, right)
    ring.wait(final.at[0, a], 4, left)
    ring.wait(final.at[1, b], 5, right)
    w = weight[...].astype(jnp.float32)
    spot = lax.broadcasted_iota(jnp.int32, (8, 48), 1) - 12 * x
    row = lax.broadcasted_iota(jnp.int32, (8, 48), 0)

    def column(b, shift, mask):
        at = jnp.logical_and(mask, spot == row + shift)
        return jnp.where(at, jnp.broadcast_to(w[b : b + 1], (8, 48)), 0.0)

    every_row = row >= 0
    root = [
        jnp.sqrt(jnp.sum(part_w, axis=1, keepdims=True))
        for part_w in (
            column(0, 0, every_row),
            column(1, 0, every_row),
            column(0, 8, row < 4) + column(1, 4, row >= 4),
        )
    ]
    mine = place.me * HELD
    margins, cross = pl.ds(0, 18), pl.ds(18, 36)
    held[pl.ds(mine, 18)] = part[x, margins] + (final[0, margins] + final[1, margins])
    cross_sum = part[x, cross] + (final[0, cross] + final[1, cross])
    for r in range(3):
        held[pl.ds(mine + 18 + 12 * r, 12)] = cross_sum[12 * r : 12 * r + 12] * root[r]

    net = Wires(send_c, recv_c)
    span = ((0, 27), (27, 27))
    pieces = (((0, 14), (14, 13)), ((27, 14), (41, 13)))

    def tiles(atom, start, count):
        return held.at[pl.ds(atom * HELD + start, count)]

    gather_plane(
        place,
        net,
        lambda h: tiles(place.me, *span[h]),
        lambda h, atom: tiles(atom, *span[h]),
        lambda h, atom, s: tiles(atom, *pieces[h][s]),
    )

    lanes = lax.broadcasted_iota(jnp.int32, (8, 128), 1)
    subs = lax.broadcasted_iota(jnp.int32, (8, 128), 0)

    def one_pair(p):
        picks = [blk[l, p] for l in range(4)]
        base = [(b // 2) * HELD for b in picks]
        par = [lax.rem(b, 2) for b in picks]
        acc = [None] * 20
        for l in range(4):
            off = picks[l] * 24
            lt = off // 128
            rem = off - lt * 128
            lm = lt - 3 * x
            hit = jnp.logical_and(lm >= 0, lm < 3)
            lm = jnp.clip(lm, 0, 2)
            turn = lax.rem(24 * l - rem + 128, 128)
            whole = lanes >= rem
            from_here = lanes >= 24 * l
            to_margin = lanes < jnp.where(hit, 24 * l + 24, 0)
            here = jnp.logical_and(from_here, lanes < 24 * l + 24)
            here_margin = jnp.logical_and(from_here, to_margin)

            def place_in(n, two, mask):
                moved = pltpu.roll(jnp.where(whole, two[0], two[1]), turn, 1)
                old = jnp.zeros_like(moved) if acc[n] is None else acc[n]
                acc[n] = jnp.where(mask, moved, old)

            for k in range(4):
                m = held[pl.ds(base[k] + par[k] * 9 + lm, 8)]
                for t in range(3):
                    place_in(3 * k + t, (m[3 * t], m[3 * t + 1]), here_margin)
                c = held[pl.ds(base[k] + 18 + par[k] * 12 + lt, 2)]
                place_in(12 + 2 * k, (c[0], c[1]), here)
                c = held[pl.ds(base[k] + 42 + lt, 2)]
                place_in(13 + 2 * k, (c[0], c[1]), here)
        limit = cabs_size[p] - 12 * x
        for k in range(4):
            first = subs < limit - 48 * k
            low = 4 * par[k]
            second = jnp.logical_and(
                jnp.logical_and(subs >= low, subs < low + 4),
                subs < limit - 48 * k - 8 + low,
            )
            acc[12 + 2 * k] = jnp.where(first, acc[12 + 2 * k], 0.0)
            acc[13 + 2 * k] = jnp.where(second, acc[13 + 2 * k], 0.0)
        margin = jnp.concatenate(acc[:12], axis=0)
        c = jnp.concatenate(acc[12:], axis=0)
        hi = c.astype(jnp.bfloat16)
        lo = (c - hi.astype(jnp.float32)).astype(jnp.bfloat16)
        prod = lax.dot_general(
            jnp.concatenate([hi, lo, hi], axis=0),
            jnp.concatenate([hi, hi, lo], axis=0),
            (((0,), (0,)), ((), ())),
            preferred_element_type=jnp.float32,
        )
        return margin - prod[:96]

    def copy_v(kind, q):
        e, o = 2 * q, 2 * q + 1
        src, dst, device = (
            lambda: (vals.at[klass(2), e], vnear.at[0, q], left),
            lambda: (vals.at[klass(2), o], vnear.at[1, q], right),
            lambda: (vals.at[klass(-1), o], vfinal.at[0, o], left),
            lambda: (vals.at[klass(1), e], vfinal.at[1, e], right),
            lambda: (vals.at[klass(-1), e], vfinal.at[0, e], left),
            lambda: (vals.at[klass(1), o], vfinal.at[1, o], right),
        )[kind]()
        at = kind * 8 + q
        return pltpu.make_async_remote_copy(
            src_ref=src, dst_ref=dst, send_sem=send_d.at[at], recv_sem=recv_d.at[at],
            device_id=device, device_id_type=MESH,
        )

    def second_step(q):
        e, o = 2 * q, 2 * q + 1
        copy_v(0, q).wait_recv()
        vals[klass(-1), e] = vals[klass(-1), e] + vnear[0, q]
        copy_v(4, q).start()
        copy_v(1, q).wait_recv()
        vals[klass(1), o] = vals[klass(1), o] + vnear[1, q]
        copy_v(5, q).start()

    wide = lax.broadcasted_iota(jnp.int32, (96, 128), 1)

    @pl.loop(0, 8)
    def _(q):
        @pl.loop(0, 2)
        def _(half):
            g = 2 * q + half
            v = [one_pair(g * 4 + n) for n in range(4)]
            r1 = pltpu.roll(v[1], 96, 1)
            r2 = pltpu.roll(v[2], 64, 1)
            r3 = pltpu.roll(v[3], 32, 1)
            packed = (
                jnp.where(wide < 96, v[0], r1),
                jnp.where(wide < 64, r1, r2),
                jnp.where(wide < 32, r2, r3),
            )
            for c in range(3):
                for k in range(4):
                    vals[k, g, :, 128 * c : 128 * c + 128] = packed[c][24 * k : 24 * k + 24]

        for kind in range(4):
            copy_v(kind, q).start()

        @pl.when(q > 0)
        def _():
            second_step(q - 1)

    second_step(7)

    narrow = lax.broadcasted_iota(jnp.int32, (24, 128), 1)
    deep = lax.broadcasted_iota(jnp.int32, (24, 128), 0) + 24 * x

    @pl.loop(0, 8)
    def _(q):
        for kind in range(2, 6):
            copy_v(kind, q).wait_recv()
        for half in range(2):
            g = 2 * q + half
            t = vals[x, g] + (vfinal[0, g] + vfinal[1, g])
            t0, t1, t2 = t[:, :128], t[:, 128:256], t[:, 256:]
            v = (
                t0,
                jnp.where(narrow < 32, pltpu.roll(t0, 32, 1), pltpu.roll(t1, 32, 1)),
                jnp.where(narrow < 64, pltpu.roll(t1, 64, 1), pltpu.roll(t2, 64, 1)),
                pltpu.roll(t2, 96, 1),
            )
            for n in range(4):
                size = pao_size[g * 4 + n]
                keep = jnp.logical_and(deep < size, narrow < size)
                out[g * 4 + n] = jnp.where(keep, v[n], 0.0)[:, :96]

    @pl.loop(0, 8)
    def _(q):
        for kind in range(6):
            copy_v(kind, q).wait_send()

    wires.drain()
    ring.drain()
    net.drain()


def fused(blk, pao_size, cabs_size, pao, cabs, weight):
    dma = pltpu.SemaphoreType.DMA
    smem = pl.BlockSpec(memory_space=pltpu.SMEM)
    vmem = pl.BlockSpec(memory_space=pltpu.VMEM)
    hbm = pl.BlockSpec(memory_space=pl.ANY)
    f32 = jnp.float32
    return pl.pallas_call(
        kernel,
        out_shape=jax.ShapeDtypeStruct((64, 24, 96), f32),
        in_specs=[smem, smem, smem, hbm, hbm, vmem],
        out_specs=vmem,
        scratch_shapes=[
            pltpu.VMEM((144, 3840), jnp.bfloat16),
            pltpu.VMEM((2, 32, 48, 1920), jnp.bfloat16),
            pltpu.VMEM((4, TILES, 8, 128), f32),
            pltpu.VMEM((2, 27, 8, 128), f32),
            pltpu.VMEM((2, TILES, 8, 128), f32),
            pltpu.VMEM((32 * HELD, 8, 128), f32),
            pltpu.VMEM((4, 16, 24, 384), f32),
            pltpu.VMEM((2, 8, 24, 384), f32),
            pltpu.VMEM((2, 16, 24, 384), f32),
            dma((2 * PER_HALF,)),
            dma((2 * PER_HALF,)),
            dma((6,)),
            dma((6,)),
            dma((2 * PER_HALF,)),
            dma((2 * PER_HALF,)),
            dma((48,)),
            dma((48,)),
            dma((4,)),
        ],
        compiler_params=pltpu.CompilerParams(
            collective_id=0, has_side_effects=True, vmem_limit_bytes=56 * 1024 * 1024
        ),
        name="fused",
    )(blk, pao_size, cabs_size, pao, cabs, weight)


def shards(pao_blocks, cabs_blocks, cabs_weight, pair_blocks, pao_size, cabs_size):
    return fused(
        pair_blocks.T,
        pao_size,
        cabs_size,
        pao_blocks.reshape(48, -1),
        cabs_blocks.reshape(96, -1),
        cabs_weight,
    )


def solution(mesh):
    placed = (
        P("atom", None, "aux"),
        P("atom", None, "aux"),
        P("atom", None),
        P("atom", None),
        P("atom"),
        P("atom"),
    )
    return jax.shard_map(
        shards, mesh=mesh, in_specs=placed, out_specs=P("atom", "aux", None), check_vma=False
    )
```

time: 158 us -> 111 us (0.70)
  waiting for transfers between devices: 27.8 us -> 0 us
  between operations: 13.6 us -> 0.01 us
  local copies, waits for them, and re-layouts: 10 us -> 2.06 us
  Pallas kernels: 104 us -> 107 us
  other arithmetic: 1.74 us -> 0 us
    reduce_scatter x1 -> x0, waiting for transfers between devices: 27.8 us -> none  [shards(): rows = lax.psum_scatter(parts, 'aux', scatter_dimension=1, tiled=True)]
    pallas_call x2 -> x1, Pallas kernels: 104 us -> 107 us  [fused(): pl.pallas_call(kernel, out_shape=jax.ShapeDtypeStruct((64, 24, 96), f32),...]
    slice x3 -> x0, local copies, waits for them, and re-layouts: 2.46 us -> none
    broadcast_in_dim x2 -> x0, local copies, waits for them, and re-layouts: 2 us -> none  [shards(): scale = jnp.broadcast_to(scale[:, :, None], (64, 64, 128))]
    unnamed x12 -> x1, local copies, waits for them, and re-layouts: 3.19 us -> 2.06 us
  transfers between devices with their start and end apart: 1 -> 0, of which waited for: 1 -> 0; matrix products, arithmetic and copies ran while one was open for 0% -> 0% of each run, Pallas kernels for 0% -> 0%
where the time goes in v3:
time: 111 us; the launch traced here: 109 us
  Pallas kernels  107 us (96%)
  local copies, waits for them, and re-layouts  2.06 us (2%)
    pallas_call x1, Pallas kernels, fused(): pl.pallas_call(kernel, out_shape=jax.ShapeDtypeStruct((64, 24, 96), f32),...  107 us

profile of v3, /device:TPU:1, one launch (start us, length us, event | category | flops | bytes accessed | tf_op | source)
XLA Modules:
  0.0 109.2 jit_solution(16909173385252814160)
XLA Ops:
  0.0 107.2 %fused.1 = f32[64,24,96]{2,1,0:T(8,128)} custom-call(s32[4,64]{1,0:T(4,128)} %bitcast.5, s32[64]{0:T(128)} %pao_size.1, s32[64]{0:T(128)} %cabs_size.1, bf16[48,3840]{1,0:T(8,128)(2,1)} %bitcast.4, bf16[96,3840]{1,0:T(8,128)(2,1)} %bitcast.3, bf16[2,48]{1,0:T(2,128)(2,1)} %weight.1), custom_call_target="tpu_custom_call" | custom-call | tf_op jit(solution)/shard_map/fused/pallas_call | solution.py:420
  107.2 2.1 %copy.8 = f32[64,24,96]{2,1,0:T(8,128)} copy(f32[64,24,96]{2,1,0:T(8,128)} %fused.1) | data formatting | bytes 1179648

commit v4 on v3

v4 whole, which is shorter than its diff:
```python
import jax
import jax.numpy as jnp
from jax import lax
from jax.experimental import pallas as pl
from jax.experimental.pallas import tpu as pltpu
from jax.sharding import PartitionSpec as P

MESH = pl.DeviceIdType.MESH

PART = 27
HELD = 2 * PART + 1

class Place:
    def __init__(self):
        self.me = lax.axis_index("atom")
        self.x = lax.axis_index("aux")
        self.core = lax.rem(self.me, 2)
        self.z = lax.rem(self.me // 2, 4)
        self.y = self.me // 8

    def atom(self, y=0, z=0, flip=False):
        core = 1 - self.core if flip else self.core
        return (lax.rem(self.y + y + 4, 4) * 4 + lax.rem(self.z + z + 4, 4)) * 2 + core

    def along(self, axis, step):
        at = self.atom(**{axis: step})
        return (at, self.x)

    def partner(self):
        return (self.atom(flip=True), self.x)

    def beside(self, step):
        return (self.me, lax.rem(self.x + step + 4, 4))


def greet(devices):
    barrier = pltpu.get_barrier_semaphore()
    for device in devices:
        pl.semaphore_signal(barrier, inc=1, device_id=device, device_id_type=MESH)
    pl.semaphore_wait(barrier, len(devices))


class Wires:
    def __init__(self, send_sem, recv_sem, first=0):
        self.send_sem, self.recv_sem, self.first = send_sem, recv_sem, first

    def copy(self, src, dst, at, device):
        return pltpu.make_async_remote_copy(
            src_ref=src,
            dst_ref=dst,
            send_sem=self.send_sem,
            recv_sem=self.recv_sem.at[self.first + at],
            device_id=device,
            device_id_type=MESH,
        )

    def send(self, src, dst, at, device):
        self.copy(src, dst, at, device).start()

    def wait(self, view, at, device):
        self.copy(view, view, at, device).wait_recv()

    def drain(self, view, device):
        self.copy(view, view, 0, device).wait_send()


OFFSETS = (0, -1, 1, 2)
AXES = (("z", "y"), ("y", "z"))


class Gather:
    BASE = 15
    TOTAL = 2 * BASE

    def __init__(self, place, wires, own, full, sub, group):
        self.place, self.wires, self.own = place, wires, own
        self.full, self.sub, self.group = full, sub, group

    def origin(self, h, k, m):
        first, second = AXES[h]
        return self.place.atom(**{first: OFFSETS[k], second: OFFSETS[m]})

    def chunk(self, h, k, m):
        return self.full(h, self.origin(h, k, m))

    def to(self, h, order, step):
        return self.place.along(AXES[h][order], step)

    def source(self, h, k, m):
        return self.own(h) if (k, m) == (0, 0) else self.chunk(h, k, m)

    def across(self, h, k, m):
        self.wires.send(
            self.source(h, k, m), self.chunk(h, k, m),
            self.TOTAL + self.group(h, k, m), self.place.partner(),
        )

    def spread(self, h, k):
        src, dst = self.source(h, k, 0), self.chunk(h, k, 0)
        at = self.BASE * h + 3 + 3 * k
        self.wires.send(src, dst, at, self.to(h, 1, 1))
        self.wires.send(src, dst, at + 1, self.to(h, 1, -1))

    def start(self):
        for h in (0, 1):
            at = self.BASE * h
            self.wires.send(self.own(h), self.chunk(h, 0, 0), at, self.to(h, 0, 1))
            self.wires.send(self.own(h), self.chunk(h, 0, 0), at + 1, self.to(h, 0, -1))
        for h in (0, 1):
            self.spread(h, 0)
            self.across(h, 0, 0)

    def hop1(self, h):
        for s, step in ((0, 1), (1, -1)):
            self.wires.wait(self.chunk(h, s + 1, 0), self.BASE * h + s, self.to(h, 0, step))

    def relay1(self, h):
        for s, step in ((0, 1), (1, -1)):
            piece = self.sub(h, self.origin(h, s + 1, 0), s)
            self.wires.send(piece, piece, self.BASE * h + 2, self.to(h, 0, step))

    def last1(self, h):
        self.wires.wait(self.chunk(h, 3, 0), self.BASE * h + 2, self.to(h, 0, 1))

    def hop2(self, h, k):
        at = self.BASE * h + 3 + 3 * k
        for s, step in ((0, 1), (1, -1)):
            self.wires.wait(self.chunk(h, k, s + 1), at + s, self.to(h, 1, step))

    def relay2(self, h, k):
        at = self.BASE * h + 5 + 3 * k
        for s, step in ((0, 1), (1, -1)):
            piece = self.sub(h, self.origin(h, k, s + 1), s)
            self.wires.send(piece, piece, at, self.to(h, 1, step))
        for s in (0, 1):
            self.across(h, k, s + 1)

    def last2(self, h, k):
        self.wires.wait(
            self.chunk(h, k, 3), self.BASE * h + 5 + 3 * k, self.to(h, 1, 1)
        )
        self.across(h, k, 3)

    def step_a(self):
        for h in (0, 1):
            self.hop1(h)
            self.relay1(h)
        for h in (0, 1):
            for k in (1, 2):
                self.spread(h, k)
                self.across(h, k, 0)

    def step_b(self):
        for h in (0, 1):
            self.hop2(h, 0)
            self.relay2(h, 0)

    def step_c(self):
        for h in (0, 1):
            self.last1(h)
            self.spread(h, 3)
            self.across(h, 3, 0)

    def step_d(self, k):
        for h in (0, 1):
            self.hop2(h, k)
            self.relay2(h, k)

    def step_e(self):
        for k in range(4):
            for h in (0, 1):
                self.last2(h, k)


class RingSum:
    def __init__(self, place, wires, part, near, final):
        self.place, self.wires = place, wires
        self.part, self.near, self.final = part, near, final
        self.left, self.right = place.beside(-1), place.beside(1)

    def klass(self, step):
        return lax.rem(self.place.x + step + 4, 4)

    def begin(self):
        a, b = pl.ds(0, 14), pl.ds(14, 13)
        send, part = self.wires.send, self.part
        send(part(self.klass(2), a), self.near.at[0, a], 0, self.left)
        send(part(self.klass(2), b), self.near.at[1, pl.ds(0, 13)], 1, self.right)
        send(part(self.klass(-1), b), self.final.at[0, b], 2, self.left)
        send(part(self.klass(1), a), self.final.at[1, a], 2, self.right)

    def middle(self):
        a, b = pl.ds(0, 14), pl.ds(14, 13)
        self.wires.wait(self.near.at[0, a], 0, self.left)
        mine = self.part(self.klass(-1), a)
        mine[...] = mine[...] + self.near[0]
        self.wires.send(mine, self.final.at[0, a], 2, self.left)
        self.wires.wait(self.near.at[1, pl.ds(0, 13)], 1, self.right)
        mine = self.part(self.klass(1), b)
        mine[...] = mine[...] + self.near[1, 0:13]
        self.wires.send(mine, self.final.at[1, b], 2, self.right)

    def finish(self):
        self.wires.wait(self.final, 2, self.left)
        own = self.part(self.place.x, pl.ds(0, PART))
        return own[...] + (self.final[0] + self.final[1])


def kernel(
    blk, pao_size, cabs_size, pao, cabs, weight, out,
    own, every, parts, near, final, held, vals, vnear, vfinal,
    send_a, recv_a, send_b, recv_b, send_c, recv_c, send_v, recv_v, local,
):
    place = Place()
    x = place.x
    load = [
        pltpu.make_async_copy(pao, own.at[pl.ds(0, 48)], local.at[0]),
        pltpu.make_async_copy(cabs, own.at[pl.ds(48, 96)], local.at[1]),
    ] + [
        pltpu.make_async_copy(
            pao.at[:, pl.ds(1920 * h, 1920)], every.at[32 * h + place.me], local.at[2 + h]
        )
        for h in range(2)
    ]
    for copy in load:
        copy.start()
    greet(
        [place.along(a, s) for a in ("y", "z") for s in (1, -1)]
        + [place.partner(), place.beside(1), place.beside(-1)]
    )
    load[0].wait()
    cuts = ((0, 1024), (1024, 896))
    first = Gather(
        place,
        Wires(send_a, recv_a),
        lambda h: own.at[pl.ds(0, 48), pl.ds(1920 * h, 1920)],
        lambda h, atom: every.at[32 * h + atom],
        lambda h, atom, s: every.at[32 * h + atom, :, pl.ds(*cuts[s])],
        lambda h, k, m: m if h == 0 else k,
    )
    sums = [
        RingSum(
            place,
            Wires(send_b.at[r], recv_b, 3 * r),
            lambda k, span, r=r: parts.at[r, k, span],
            near.at[r],
            final.at[r],
        )
        for r in range(2)
    ]

    def tiles(atom, start, count):
        return held.at[pl.ds(atom * HELD + start, count)]

    span = ((0, 14), (14, 13))
    pieces = (((0, 7), (7, 7)), ((14, 7), (21, 6)))
    nets = [
        Gather(
            place,
            Wires(send_c.at[r], recv_c, 31 * r),
            lambda h, r=r: tiles(place.me, PART * r + span[h][0], span[h][1]),
            lambda h, atom, r=r: tiles(atom, PART * r + span[h][0], span[h][1]),
            lambda h, atom, s, r=r: tiles(
                atom, PART * r + pieces[h][s][0], pieces[h][s][1]
            ),
            lambda h, k, m: 0,
        )
        for r in range(2)
    ]

    first.start()

    w = weight[...].astype(jnp.float32)
    spot = lax.broadcasted_iota(jnp.int32, (8, 48), 1) - 12 * x
    row = lax.broadcasted_iota(jnp.int32, (8, 48), 0)

    def column(b, shift, mask):
        at = jnp.logical_and(mask, spot == row + shift)
        return jnp.where(at, jnp.broadcast_to(w[b : b + 1], (8, 48)), 0.0)

    root = [
        jnp.sqrt(jnp.sum(part_w, axis=1, keepdims=True))
        for part_w in (
            column(0, 0, row >= 0),
            column(1, 0, row >= 0),
            column(0, 8, row < 4) + column(1, 4, row >= 4),
        )
    ]

    nt = (((1,), (1,)), ((), ()))

    def line_products(step, slot):
        line = lax.rem(place.y + step + 4, 4)
        first.wires.wait(every.at[pl.ds(0, 8)], first.TOTAL + OFFSETS.index(step), place.partner())
        g = None
        for h in range(2):
            rows = every[pl.ds(32 * h + line * 8, 8)].reshape(384, 1920)
            d = lax.dot_general(
                own[:, 1920 * h : 1920 * (h + 1)], rows, nt,
                preferred_element_type=jnp.float32,
            )
            g = d if g is None else g + d
        r, start = (0, 9 * slot) if slot < 3 else (1, 0)
        for c in range(3):
            col = g[:, 128 * c : 128 * c + 128]
            for t in range(6):
                parts[1, line, 9 + t * 3 + c] = col[8 * t : 8 * t + 8]
            for k in range(4):
                a, b = 48 + 12 * k, 96 + 12 * k
                parts[r, k, start + c] = col[a : a + 8]
                parts[r, k, start + 3 + c] = col[b : b + 8]
                parts[r, k, start + 6 + c] = jnp.concatenate(
                    [col[a + 8 : a + 12], col[b + 8 : b + 12]], axis=0
                )

    mine = place.me * HELD

    def keep_part(r):
        total = sums[r].finish()
        for n in range(9):
            if r == 0 or n < 3:
                held[pl.ds(mine + PART * r + 3 * n, 3)] = total[3 * n : 3 * n + 3] * root[n % 3]
        if r == 1:
            held[pl.ds(mine + PART + 9, 18)] = total[9:]

    first.hop1(0)
    first.relay1(0)
    for k in (1, 2):
        first.spread(0, k)
        first.across(0, k, 0)
    first.hop1(1)
    for k in (1, 2):
        first.spread(1, k)
        first.across(1, k, 0)
    first.last1(0)
    first.spread(0, 3)
    first.across(0, 3, 0)
    first.relay1(1)
    first.hop2(1, 0)
    first.relay2(1, 0)
    for copy in load[1:]:
        copy.wait()
    first.hop2(0, 0)
    first.relay2(0, 0)
    for k in (1, 2):
        first.hop2(1, k)
        first.relay2(1, k)
        first.hop2(0, k)
        first.relay2(0, k)
    first.last2(1, 0)
    line_products(0, 0)
    first.last1(1)
    first.spread(1, 3)
    first.across(1, 3, 0)
    first.hop2(0, 3)
    first.relay2(0, 3)
    first.last2(1, 1)
    first.last2(1, 2)
    line_products(1, 1)
    line_products(-1, 2)
    sums[0].begin()
    first.last2(0, 0)
    first.hop2(1, 3)
    first.relay2(1, 3)
    first.last2(0, 1)
    first.last2(0, 2)
    sums[0].middle()
    first.last2(0, 3)
    first.last2(1, 3)
    keep_part(0)
    nets[0].start()
    line_products(2, 3)
    sums[1].begin()
    nets[0].step_a()
    sums[1].middle()
    nets[0].step_b()
    nets[0].step_c()
    keep_part(1)
    nets[1].start()
    nets[0].step_d(1)
    nets[0].step_d(2)
    nets[1].step_a()
    nets[0].step_d(3)
    nets[1].step_b()
    nets[1].step_c()
    nets[0].step_e()
    for k in (1, 2, 3):
        nets[1].step_d(k)
    nets[1].step_e()
    for r in range(2):
        nets[r].wires.wait(held.at[pl.ds(0, 16 * PART)], nets[r].TOTAL, place.partner())

    lanes = lax.broadcasted_iota(jnp.int32, (8, 128), 1)
    subs = lax.broadcasted_iota(jnp.int32, (8, 128), 0)

    def half_of(n, bits):
        return lax.shift_right_logical(n, jnp.int32(bits))

    def one_pair(p):
        picks = [blk[l, p] for l in range(4)]
        base = [half_of(b, 1) * HELD for b in picks]
        par = [jnp.bitwise_and(b, 1) for b in picks]
        lines = [half_of(b, 4) for b in picks]
        acc = [None] * 20
        for l in range(4):
            off = jnp.bitwise_and(picks[l], 15) * 24
            u = half_of(off, 7)
            rem = jnp.bitwise_and(off, 127)
            turn = jnp.bitwise_and(24 * l + 128 - rem, 127)
            whole = lanes >= rem
            from_here = lanes >= 24 * l
            to_margin = lanes < jnp.where(lines[l] == x, 24 * l + 24, 0)
            here = jnp.logical_and(from_here, lanes < 24 * l + 24)
            here_margin = jnp.logical_and(from_here, to_margin)

            def place_in(n, two, mask):
                moved = pltpu.roll(jnp.where(whole, two[0], two[1]), turn, 1)
                old = jnp.zeros_like(moved) if acc[n] is None else acc[n]
                acc[n] = jnp.where(mask, moved, old)

            for k in range(4):
                m = held[pl.ds(base[k] + par[k] * 9 + (u + PART + 9), 8)]
                for t in range(3):
                    place_in(3 * k + t, (m[3 * t], m[3 * t + 1]), here_margin)
                away = jnp.bitwise_and(lines[l] - lines[k], 3)
                at = base[k] + jnp.bitwise_xor(away, half_of(away, 1)) * 9 + u
                c = held[pl.ds(at + par[k] * 3, 2)]
                place_in(12 + 2 * k, (c[0], c[1]), here)
                c = held[pl.ds(at + 6, 2)]
                place_in(13 + 2 * k, (c[0], c[1]), here)
        limit = cabs_size[p] - 12 * x
        for k in range(4):
            first = subs < limit - 48 * k
            low = 4 * par[k]
            second = jnp.logical_and(
                jnp.logical_and(subs >= low, subs < low + 4),
                subs < limit - 48 * k - 8 + low,
            )
            acc[12 + 2 * k] = jnp.where(first, acc[12 + 2 * k], 0.0)
            acc[13 + 2 * k] = jnp.where(second, acc[13 + 2 * k], 0.0)
        margin = jnp.concatenate(acc[:12], axis=0)
        c = jnp.concatenate(acc[12:], axis=0)
        hi = c.astype(jnp.bfloat16)
        lo = (c - hi.astype(jnp.float32)).astype(jnp.bfloat16)
        prod = lax.dot_general(
            jnp.concatenate([hi, lo, hi], axis=0),
            jnp.concatenate([hi, hi, lo], axis=0),
            (((0,), (0,)), ((), ())),
            preferred_element_type=jnp.float32,
        )
        return margin - prod[:96]

    left, right = place.beside(-1), place.beside(1)
    klass = sums[0].klass

    def copy_v(kind, q):
        e, o = 2 * q, 2 * q + 1
        src, dst, device, at = (
            lambda: (vals.at[klass(2) * 16 + e], vnear.at[2 * q], left, 3 * q),
            lambda: (vals.at[klass(2) * 16 + o], vnear.at[2 * q + 1], right, 3 * q + 1),
            lambda: (vals.at[klass(-1) * 16 + o], vfinal.at[o], left, 3 * q + 2),
            lambda: (vals.at[klass(1) * 16 + e], vfinal.at[16 + e], right, 3 * q + 2),
            lambda: (vals.at[klass(-1) * 16 + e], vfinal.at[e], left, 3 * q + 2),
            lambda: (vals.at[klass(1) * 16 + o], vfinal.at[16 + o], right, 3 * q + 2),
        )[kind]()
        return Wires(send_v, recv_v).copy(src, dst, at, device)

    def second_step(q):
        e, o = klass(-1) * 16 + 2 * q, klass(1) * 16 + 2 * q + 1
        copy_v(0, q).wait_recv()
        vals[e] = vals[e] + vnear[2 * q]
        copy_v(4, q).start()
        copy_v(1, q).wait_recv()
        vals[o] = vals[o] + vnear[2 * q + 1]
        copy_v(5, q).start()

    wide = lax.broadcasted_iota(jnp.int32, (96, 128), 1)

    @pl.loop(0, 8)
    def _(q):
        @pl.loop(0, 2)
        def _(half):
            g = 2 * q + half
            v = [one_pair(g * 4 + n) for n in range(4)]
            r1 = pltpu.roll(v[1], 96, 1)
            r2 = pltpu.roll(v[2], 64, 1)
            r3 = pltpu.roll(v[3], 32, 1)
            packed = (
                jnp.where(wide < 96, v[0], r1),
                jnp.where(wide < 64, r1, r2),
                jnp.where(wide < 32, r2, r3),
            )
            for c in range(3):
                for k in range(4):
                    vals[k * 16 + g, :, 128 * c : 128 * c + 128] = packed[c][24 * k : 24 * k + 24]

        for kind in range(4):
            copy_v(kind, q).start()

        @pl.when(q > 0)
        def _():
            second_step(q - 1)

    second_step(7)

    narrow = lax.broadcasted_iota(jnp.int32, (24, 128), 1)
    deep = lax.broadcasted_iota(jnp.int32, (24, 128), 0) + 24 * x

    @pl.loop(0, 8)
    def _(q):
        view = vfinal.at[pl.ds(0, 4)]
        Wires(send_v, recv_v).wait(view, 3 * q + 2, left)
        for half in range(2):
            g = 2 * q + half
            t = vals[x * 16 + g] + (vfinal[g] + vfinal[16 + g])
            t0, t1, t2 = t[:, :128], t[:, 128:256], t[:, 256:]
            v = (
                t0,
                jnp.where(narrow < 32, pltpu.roll(t0, 32, 1), pltpu.roll(t1, 32, 1)),
                jnp.where(narrow < 64, pltpu.roll(t1, 64, 1), pltpu.roll(t2, 64, 1)),
                pltpu.roll(t2, 96, 1),
            )
            for n in range(4):
                size = pao_size[g * 4 + n]
                keep = jnp.logical_and(deep < size, narrow < size)
                out[g * 4 + n] = jnp.where(keep, v[n], 0.0)[:, :96]

    first.wires.drain(every.at[pl.ds(0, 62)], left)
    for r in range(2):
        sums[r].wires.drain(held.at[pl.ds(0, 3 * PART)], left)
        nets[r].wires.drain(held.at[pl.ds(0, 31 * PART)], left)
    Wires(send_v, recv_v).drain(vals.at[pl.ds(0, 48)], left)


def fused(blk, pao_size, cabs_size, pao, cabs, weight):
    dma = pltpu.SemaphoreType.DMA
    smem = pl.BlockSpec(memory_space=pltpu.SMEM)
    vmem = pl.BlockSpec(memory_space=pltpu.VMEM)
    hbm = pl.BlockSpec(memory_space=pl.ANY)
    f32 = jnp.float32
    return pl.pallas_call(
        kernel,
        out_shape=jax.ShapeDtypeStruct((64, 24, 96), f32),
        in_specs=[smem, smem, smem, hbm, hbm, vmem],
        out_specs=vmem,
        scratch_shapes=[
            pltpu.VMEM((144, 3840), jnp.bfloat16),
            pltpu.VMEM((64, 48, 1920), jnp.bfloat16),
            pltpu.VMEM((2, 4, PART, 8, 128), f32),
            pltpu.VMEM((2, 2, 14, 8, 128), f32),
            pltpu.VMEM((2, 2, PART, 8, 128), f32),
            pltpu.VMEM((32 * HELD, 8, 128), f32),
            pltpu.VMEM((64, 24, 384), f32),
            pltpu.VMEM((16, 24, 384), f32),
            pltpu.VMEM((32, 24, 384), f32),
            dma,
            dma((Gather.TOTAL + 4,)),
            dma((2,)),
            dma((6,)),
            dma((2,)),
            dma((2 * Gather.TOTAL + 2,)),
            dma,
            dma((24,)),
            dma((4,)),
        ],
        compiler_params=pltpu.CompilerParams(
            collective_id=0, has_side_effects=True, vmem_limit_bytes=56 * 1024 * 1024
        ),
        name="fused",
    )(blk, pao_size, cabs_size, pao, cabs, weight)


def shards(pao_blocks, cabs_blocks, cabs_weight, pair_blocks, pao_size, cabs_size):
    return fused(
        pair_blocks.T,
        pao_size,
        cabs_size,
        pao_blocks.reshape(48, -1),
        cabs_blocks.reshape(96, -1),
        cabs_weight,
    )


def solution(mesh):
    placed = (
        P("atom", None, "aux"),
        P("atom", None, "aux"),
        P("atom", None),
        P("atom", None),
        P("atom"),
        P("atom"),
    )
    return jax.shard_map(
        shards, mesh=mesh, in_specs=placed, out_specs=P("atom", "aux", None), check_vma=False
    )
```

time: 111 us -> 101 us (0.910)
  Pallas kernels: 107 us -> 97.6 us
    pallas_call x1, Pallas kernels: 107 us -> 97.6 us  [fused(): pl.pallas_call(kernel, out_shape=jax.ShapeDtypeStruct((64, 24, 96), f32),...]
where the time goes in v4:
time: 101 us; the launch traced here: 99.6 us
  Pallas kernels  97.6 us (97%)
  local copies, waits for them, and re-layouts  2.06 us (2%)
    pallas_call x1, Pallas kernels, fused(): pl.pallas_call(kernel, out_shape=jax.ShapeDtypeStruct((64, 24, 96), f32),...  97.6 us
    unnamed x1, local copies, waits for them, and re-layouts  2.06 us

profile of v4, /device:TPU:1, one launch (start us, length us, event | category | flops | bytes accessed | tf_op | source)
XLA Modules:
  0.0 99.6 jit_solution(13426934221944108955)
XLA Ops:
  0.0 97.6 %fused.1 = f32[64,24,96]{2,1,0:T(8,128)} custom-call(s32[4,64]{1,0:T(4,128)} %bitcast.5, s32[64]{0:T(128)} %pao_size.1, s32[64]{0:T(128)} %cabs_size.1, bf16[48,3840]{1,0:T(8,128)(2,1)} %bitcast.4, bf16[96,3840]{1,0:T(8,128)(2,1)} %bitcast.3, bf16[2,48]{1,0:T(2,128)(2,1)} %weight.1), custom_call_target="tpu_custom_call" | custom-call | tf_op jit(solution)/shard_map/fused/pallas_call | solution.py:541
  97.6 2.1 %copy.8 = f32[64,24,96]{2,1,0:T(8,128)} copy(f32[64,24,96]{2,1,0:T(8,128)} %fused.1) | data formatting | bytes 1179648

commit v5 on v4

v5 whole, which is shorter than its diff:
```python
import jax
import jax.numpy as jnp
from jax import lax
from jax.experimental import pallas as pl
from jax.experimental.pallas import tpu as pltpu
from jax.sharding import PartitionSpec as P

MESH = pl.DeviceIdType.MESH

PARTS = (((0, 2), 0, 18), ((1,), 18, 9), ((3,), 27, 9), )
HELD = 37
CHOSEN = 577

START, RELAY, SPREAD, PASS, ACROSS, LINE = range(6)
FAR, PLAIN, MIXED, KEEP, PICK, BLOCK = range(6, 12)

ORDER = (
    (START, 0, 0, 0), (START, 0, 0, 1), (START, 0, 1, 0), (START, 0, 1, 1),
    (ACROSS, 0, 1, 0, 0), (ACROSS, 0, 0, 0, 0), (SPREAD, 0, 1, 0, 0),
    (SPREAD, 0, 1, 0, 1), (SPREAD, 0, 0, 0, 0), (SPREAD, 0, 0, 0, 1),
    (ACROSS, 0, 1, 2, 0), (ACROSS, 0, 1, 1, 0), (ACROSS, 0, 0, 1, 0), (RELAY, 0, 0, 0),
    (RELAY, 0, 0, 1), (RELAY, 0, 1, 0), (RELAY, 0, 1, 1), (ACROSS, 0, 0, 2, 0),
    (SPREAD, 0, 1, 2, 0), (SPREAD, 0, 1, 2, 1), (SPREAD, 0, 0, 1, 0),
    (SPREAD, 0, 0, 2, 1), (ACROSS, 0, 1, 0, 1), (ACROSS, 0, 1, 0, 2),
    (ACROSS, 0, 0, 0, 2), (ACROSS, 0, 0, 0, 1), (ACROSS, 0, 1, 3, 0),
    (ACROSS, 0, 0, 3, 0), (PASS, 0, 1, 0, 0), (PASS, 0, 1, 0, 1), (PASS, 0, 0, 0, 0),
    (SPREAD, 0, 0, 3, 1), (SPREAD, 0, 1, 1, 0), (SPREAD, 0, 1, 1, 1),
    (SPREAD, 0, 0, 3, 0), (ACROSS, 0, 1, 2, 2), (ACROSS, 0, 0, 2, 2),
    (ACROSS, 0, 0, 1, 1), (SPREAD, 0, 0, 1, 1), (ACROSS, 0, 1, 2, 1),
    (ACROSS, 0, 1, 0, 3), (PASS, 0, 1, 2, 0), (PASS, 0, 1, 2, 1), (SPREAD, 0, 0, 2, 0),
    (ACROSS, 0, 0, 3, 2), (LINE, 0), (SPREAD, 0, 1, 3, 0), (SPREAD, 0, 1, 3, 1),
    (PASS, 0, 0, 0, 1), (PICK, 0), (ACROSS, 0, 1, 1, 1), (ACROSS, 0, 1, 1, 2),
    (ACROSS, 0, 0, 3, 1), (PASS, 0, 0, 1, 0), (PASS, 0, 0, 3, 1), (ACROSS, 0, 1, 2, 3),
    (ACROSS, 0, 0, 1, 2), (PASS, 0, 1, 1, 0), (PASS, 0, 1, 1, 1), (PASS, 0, 0, 3, 0),
    (PASS, 0, 0, 1, 1), (ACROSS, 0, 0, 0, 3), (LINE, 2), (ACROSS, 0, 0, 2, 1),
    (PLAIN, 0, 1), (FAR, 0, 0), (PASS, 0, 0, 2, 0), (PASS, 0, 0, 2, 1), (PICK, 2),
    (PASS, 0, 1, 3, 0), (PASS, 0, 1, 3, 1), (ACROSS, 0, 1, 3, 2), (FAR, 0, 1),
    (PLAIN, 0, 0), (ACROSS, 0, 1, 3, 1), (ACROSS, 0, 1, 1, 3), (MIXED, 0, 0),
    (ACROSS, 0, 0, 3, 3), (MIXED, 0, 1), (ACROSS, 0, 0, 1, 3), (LINE, 1),
    (ACROSS, 0, 0, 2, 3), (FAR, 1, 1), (FAR, 1, 0), (ACROSS, 0, 1, 3, 3),
    (PLAIN, 1, 1), (PLAIN, 1, 0), (PICK, 1), (BLOCK, 0, 0), (BLOCK, 0, 1),
    (KEEP, 0), (SPREAD, 1, 1, 0, 0), (START, 1, 0, 1), (START, 1, 1, 0),
    (START, 1, 1, 1), (ACROSS, 1, 0, 0, 0), (LINE, 3), (ACROSS, 1, 1, 0, 0),
    (FAR, 2, 1), (FAR, 2, 0), (START, 1, 0, 0), (SPREAD, 1, 1, 0, 1),
    (SPREAD, 1, 0, 0, 0), (SPREAD, 1, 0, 0, 1), (PLAIN, 2, 1), (MIXED, 1, 0),
    (MIXED, 1, 1), (PLAIN, 2, 0), (PICK, 3), (BLOCK, 1, 0), (BLOCK, 1, 1),
    (SPREAD, 1, 1, 2, 0), (RELAY, 1, 0, 1), (RELAY, 1, 1, 0), (RELAY, 1, 1, 1),
    (ACROSS, 1, 1, 1, 0), (ACROSS, 1, 1, 2, 0), (ACROSS, 1, 1, 0, 1),
    (ACROSS, 1, 0, 2, 0), (MIXED, 2, 1), (MIXED, 2, 0), (SPREAD, 1, 1, 1, 1),
    (SPREAD, 1, 0, 2, 0), (SPREAD, 1, 0, 2, 1), (RELAY, 1, 0, 0), (ACROSS, 1, 0, 1, 0),
    (ACROSS, 1, 0, 0, 2), (ACROSS, 1, 1, 0, 2), (ACROSS, 1, 0, 0, 1), (KEEP, 1),
    (SPREAD, 1, 1, 1, 0), (SPREAD, 1, 1, 2, 1), (SPREAD, 1, 0, 1, 0),
    (SPREAD, 1, 0, 1, 1), (ACROSS, 2, 0, 0, 0), (ACROSS, 2, 1, 0, 0), (START, 2, 0, 0),
    (START, 2, 0, 1), (START, 2, 1, 0), (START, 2, 1, 1), (SPREAD, 2, 0, 0, 0),
    (SPREAD, 2, 0, 0, 1), (SPREAD, 2, 1, 0, 0), (SPREAD, 2, 1, 0, 1), (BLOCK, 2, 0),
    (BLOCK, 2, 1), (ACROSS, 1, 1, 3, 0), (SPREAD, 1, 1, 3, 0), (SPREAD, 1, 1, 3, 1),
    (PASS, 1, 0, 0, 0), (PASS, 1, 0, 0, 1), (KEEP, 2), (ACROSS, 1, 1, 2, 1),
    (START, 3, 1, 0), (START, 3, 1, 1), (ACROSS, 3, 0, 0, 0), (ACROSS, 3, 1, 0, 0),
    (ACROSS, 1, 1, 1, 2), (START, 3, 0, 0), (START, 3, 0, 1), (SPREAD, 1, 0, 3, 0),
    (SPREAD, 1, 0, 3, 1), (ACROSS, 1, 0, 3, 0), (ACROSS, 1, 0, 2, 1),
    (ACROSS, 1, 0, 2, 2), (SPREAD, 3, 1, 0, 0), (SPREAD, 3, 1, 0, 1), (BLOCK, 3, 0),
    (ACROSS, 1, 0, 1, 1), (PASS, 1, 1, 1, 0), (PASS, 1, 1, 2, 1), (SPREAD, 3, 0, 0, 0),
    (SPREAD, 3, 0, 0, 1), (ACROSS, 1, 0, 1, 2), (ACROSS, 1, 1, 2, 2),
    (ACROSS, 2, 1, 1, 0), (ACROSS, 2, 1, 2, 0), (RELAY, 2, 0, 0), (RELAY, 2, 0, 1),
    (ACROSS, 2, 0, 2, 0), (RELAY, 2, 1, 0), (RELAY, 2, 1, 1), (ACROSS, 2, 0, 1, 0),
    (ACROSS, 1, 1, 1, 1), (SPREAD, 2, 1, 1, 0), (SPREAD, 2, 1, 2, 1),
    (SPREAD, 2, 0, 2, 0), (SPREAD, 2, 0, 1, 1), (ACROSS, 2, 0, 0, 1),
    (ACROSS, 2, 0, 0, 2), (ACROSS, 2, 1, 0, 1), (ACROSS, 2, 1, 0, 2),
    (SPREAD, 2, 1, 2, 0), (SPREAD, 2, 1, 1, 1), (SPREAD, 2, 0, 1, 0),
    (SPREAD, 2, 0, 2, 1), (BLOCK, 3, 1), (ACROSS, 1, 0, 0, 3), (PASS, 1, 1, 0, 0),
    (PASS, 1, 1, 1, 1), (ACROSS, 1, 1, 3, 1), (PASS, 1, 0, 1, 0), (PASS, 1, 0, 2, 1),
    (ACROSS, 1, 1, 3, 2), (SPREAD, 3, 1, 1, 0), (SPREAD, 3, 1, 1, 1),
    (ACROSS, 3, 1, 2, 0), (ACROSS, 3, 1, 1, 0), (RELAY, 3, 1, 0), (RELAY, 3, 1, 1),
    (ACROSS, 3, 0, 1, 0), (ACROSS, 3, 0, 2, 0), (RELAY, 3, 0, 0), (RELAY, 3, 0, 1),
    (SPREAD, 3, 0, 1, 0), (SPREAD, 3, 0, 1, 1), (SPREAD, 3, 1, 2, 0),
    (SPREAD, 3, 1, 2, 1), (ACROSS, 3, 1, 0, 1), (ACROSS, 1, 0, 3, 1),
    (ACROSS, 1, 0, 3, 2), (SPREAD, 3, 0, 2, 0), (SPREAD, 3, 0, 2, 1),
    (ACROSS, 3, 1, 0, 2), (PASS, 3, 1, 0, 0), (PASS, 3, 1, 0, 1), (BLOCK, 0, 2),
    (ACROSS, 3, 0, 0, 1), (PASS, 1, 1, 3, 0), (PASS, 1, 1, 0, 1), (ACROSS, 3, 0, 0, 2),
    (ACROSS, 2, 0, 3, 0), (PASS, 3, 0, 0, 0), (PASS, 3, 0, 0, 1), (ACROSS, 2, 1, 3, 0),
    (SPREAD, 2, 0, 3, 0), (SPREAD, 2, 0, 3, 1), (SPREAD, 2, 1, 3, 0),
    (SPREAD, 2, 1, 3, 1), (ACROSS, 2, 1, 2, 2), (ACROSS, 2, 1, 1, 1),
    (ACROSS, 2, 0, 2, 1), (ACROSS, 2, 0, 1, 2), (PASS, 1, 1, 2, 0), (PASS, 1, 1, 3, 1),
    (ACROSS, 2, 1, 2, 1), (PASS, 1, 0, 3, 0), (PASS, 1, 0, 3, 1), (ACROSS, 2, 1, 1, 2),
    (ACROSS, 2, 0, 1, 1), (ACROSS, 2, 0, 2, 2), (PASS, 2, 1, 1, 0), (PASS, 2, 1, 1, 1),
    (BLOCK, 1, 2), (ACROSS, 1, 1, 1, 3), (PASS, 1, 0, 2, 0), (PASS, 1, 0, 1, 1),
    (PASS, 2, 1, 2, 0), (PASS, 2, 1, 2, 1), (PASS, 2, 1, 0, 0), (PASS, 2, 1, 0, 1),
    (ACROSS, 3, 1, 1, 1), (ACROSS, 3, 1, 3, 0), (PASS, 2, 0, 0, 0), (PASS, 2, 0, 0, 1),
    (ACROSS, 3, 1, 1, 2), (PASS, 3, 1, 1, 0), (PASS, 3, 1, 1, 1), (ACROSS, 3, 0, 3, 0),
    (SPREAD, 3, 0, 3, 0), (SPREAD, 3, 0, 3, 1), (SPREAD, 3, 1, 3, 0),
    (SPREAD, 3, 1, 3, 1), (ACROSS, 3, 0, 1, 2), (ACROSS, 3, 0, 1, 1),
    (ACROSS, 3, 1, 2, 1), (PASS, 3, 1, 2, 0), (PASS, 3, 1, 2, 1), (ACROSS, 3, 1, 2, 2),
    (PASS, 3, 0, 1, 0), (PASS, 3, 0, 1, 1), (ACROSS, 3, 1, 0, 3), (ACROSS, 3, 0, 2, 1),
    (PASS, 3, 0, 2, 0), (PASS, 3, 0, 2, 1), (ACROSS, 3, 0, 2, 2), (BLOCK, 2, 2),
    (ACROSS, 3, 0, 0, 3), (PASS, 2, 0, 2, 0), (PASS, 2, 0, 1, 1), (ACROSS, 1, 1, 0, 3),
    (PASS, 2, 0, 1, 0), (PASS, 2, 0, 2, 1), (PASS, 2, 1, 3, 0), (PASS, 2, 1, 3, 1),
    (ACROSS, 2, 1, 3, 1), (ACROSS, 2, 1, 3, 2), (PASS, 2, 0, 3, 0), (PASS, 2, 0, 3, 1),
    (ACROSS, 2, 0, 3, 2), (ACROSS, 2, 0, 3, 1), (ACROSS, 1, 1, 2, 3),
    (ACROSS, 1, 0, 3, 3), (ACROSS, 1, 1, 3, 3), (BLOCK, 3, 2), (ACROSS, 2, 1, 2, 3),
    (ACROSS, 2, 1, 1, 3), (ACROSS, 1, 0, 1, 3), (ACROSS, 1, 0, 2, 3),
    (ACROSS, 2, 0, 0, 3), (ACROSS, 3, 1, 1, 3), (ACROSS, 2, 1, 0, 3), (BLOCK, 4, 0),
    (PASS, 3, 1, 3, 0), (PASS, 3, 1, 3, 1), (ACROSS, 3, 1, 3, 1), (ACROSS, 3, 1, 3, 2),
    (PASS, 3, 0, 3, 0), (PASS, 3, 0, 3, 1), (ACROSS, 3, 0, 3, 1), (ACROSS, 3, 0, 3, 2),
    (ACROSS, 3, 1, 2, 3), (ACROSS, 3, 0, 1, 3), (ACROSS, 3, 0, 2, 3), (BLOCK, 4, 1),
    (ACROSS, 2, 0, 2, 3), (ACROSS, 2, 0, 1, 3), (ACROSS, 2, 1, 3, 3),
    (ACROSS, 2, 0, 3, 3), (BLOCK, 4, 2), (BLOCK, 5, 0), (ACROSS, 3, 1, 3, 3),
    (ACROSS, 3, 0, 3, 3), (BLOCK, 5, 1), (BLOCK, 5, 2),
)


class Place:
    def __init__(self):
        self.me = lax.axis_index("atom")
        self.x = lax.axis_index("aux")
        self.core = lax.rem(self.me, 2)
        self.z = lax.rem(self.me // 2, 4)
        self.y = self.me // 8

    def atom(self, y=0, z=0, flip=False):
        core = 1 - self.core if flip else self.core
        return (lax.rem(self.y + y + 4, 4) * 4 + lax.rem(self.z + z + 4, 4)) * 2 + core

    def along(self, axis, step):
        at = self.atom(**{axis: step})
        return (at, self.x)

    def partner(self):
        return (self.atom(flip=True), self.x)

    def beside(self, step):
        return (self.me, lax.rem(self.x + step + 4, 4))


def greet(devices):
    barrier = pltpu.get_barrier_semaphore()
    for device in devices:
        pl.semaphore_signal(barrier, inc=1, device_id=device, device_id_type=MESH)
    pl.semaphore_wait(barrier, len(devices))


class Wires:
    def __init__(self, send_sem, recv_sem, first=0):
        self.send_sem, self.recv_sem, self.first = send_sem, recv_sem, first

    def copy(self, src, dst, at, device):
        return pltpu.make_async_remote_copy(
            src_ref=src,
            dst_ref=dst,
            send_sem=self.send_sem,
            recv_sem=self.recv_sem.at[self.first + at],
            device_id=device,
            device_id_type=MESH,
        )

    def send(self, src, dst, at, device):
        self.copy(src, dst, at, device).start()

    def wait(self, view, at, device):
        self.copy(view, view, at, device).wait_recv()

    def drain(self, view, device):
        self.copy(view, view, 0, device).wait_send()


OFFSETS = (0, -1, 1, 2)
SLOTS = (0, 2, 1, 3)
AXES = (("z", "y"), ("y", "z"))


class Gather:
    BASE = 15
    TOTAL = 2 * BASE

    def __init__(self, place, wires, own, full, sub, group):
        self.place, self.wires, self.own = place, wires, own
        self.full, self.sub, self.group = full, sub, group

    def origin(self, h, k, m):
        first, second = AXES[h]
        return self.place.atom(**{first: OFFSETS[k], second: OFFSETS[m]})

    def chunk(self, h, k, m):
        return self.full(h, self.origin(h, k, m))

    def to(self, h, order, s):
        return self.place.along(AXES[h][order], 1 - 2 * s)

    def source(self, h, k, m):
        return self.own(h) if (k, m) == (0, 0) else self.chunk(h, k, m)

    def start(self, h, s):
        self.wires.send(self.own(h), self.chunk(h, 0, 0), self.BASE * h + s, self.to(h, 0, s))

    def relay(self, h, s):
        piece = self.sub(h, self.origin(h, s + 1, 0), s)
        self.wires.send(piece, piece, self.BASE * h + 2, self.to(h, 0, s))

    def spread(self, h, k, s):
        self.wires.send(
            self.source(h, k, 0), self.chunk(h, k, 0), self.BASE * h + 3 + 3 * k + s,
            self.to(h, 1, s),
        )

    def pass_on(self, h, k, s):
        piece = self.sub(h, self.origin(h, k, s + 1), s)
        self.wires.send(piece, piece, self.BASE * h + 5 + 3 * k, self.to(h, 1, s))

    def across(self, h, k, m):
        self.wires.send(
            self.source(h, k, m), self.chunk(h, k, m),
            self.TOTAL + self.group(h, k, m), self.place.partner(),
        )

    def arrived1(self, h, s):
        self.wires.wait(self.chunk(h, s + 1, 0), self.BASE * h + s, self.to(h, 0, s))

    def arrived1s(self, h):
        self.wires.wait(self.chunk(h, 3, 0), self.BASE * h + 2, self.to(h, 0, 0))

    def arrived2(self, h, k, s):
        self.wires.wait(
            self.chunk(h, k, s + 1), self.BASE * h + 3 + 3 * k + s, self.to(h, 1, s)
        )

    def arrived2s(self, h, k):
        self.wires.wait(self.chunk(h, k, 3), self.BASE * h + 5 + 3 * k, self.to(h, 1, 0))

    def from_partner(self, view, n):
        self.wires.wait(view, self.TOTAL + n, self.place.partner())


class RingSum:
    def __init__(self, place, wires, count, part, near, final):
        self.place, self.wires, self.count = place, wires, count
        self.part, self.near, self.final = part, near, final
        half = (count + 1) // 2
        self.cut = (pl.ds(0, half), pl.ds(half, count - half))
        self.size = (half, count - half)

    def klass(self, step):
        return lax.rem(self.place.x + step + 4, 4)

    def to(self, s):
        return self.place.beside(2 * s - 1)

    def near_at(self, s):
        return self.near.at[s, pl.ds(0, self.size[s])]

    def far(self, s):
        self.wires.send(self.part(self.klass(2), self.cut[s]), self.near_at(s), s, self.to(s))

    def plain(self, s):
        cut = self.cut[1 - s]
        self.wires.send(
            self.part(self.klass(2 * s - 1), cut), self.final.at[s, cut], 2, self.to(s)
        )

    def mixed(self, s):
        cut = self.cut[s]
        mine = self.part(self.klass(2 * s - 1), cut)
        mine[...] = mine[...] + self.near[s, 0 : self.size[s]]
        self.wires.send(mine, self.final.at[s, cut], 2, self.to(s))

    def arrived(self, s):
        self.wires.wait(self.near_at(s), s, self.to(s))

    def total(self):
        self.wires.wait(self.final, 2, self.to(0))
        own = self.part(self.place.x, pl.ds(0, self.count))
        return own[...] + (self.final[0] + self.final[1])


def kernel(
    blk_in, pao_size_in, cabs_size_in, pao, cabs, weight_in, out,
    blk, pao_size, cabs_size, blk_rows, weight, own, every, chosen, margins, parts, nears, finals, held, vals, vnear, vfinal,
    send_a, recv_a, send_b, recv_b, send_c, recv_c, send_v, recv_v, local,
):
    place = Place()
    x = place.x
    load = [
        pltpu.make_async_copy(pao, own.at[pl.ds(0, 48)], local.at[0]),
        pltpu.make_async_copy(cabs, own.at[pl.ds(48, 96)], local.at[1]),
    ] + [
        pltpu.make_async_copy(
            pao.at[:, pl.ds(1920 * h, 1920)], every.at[32 * h + place.me], local.at[2 + h]
        )
        for h in range(2)
    ]
    load += [
        pltpu.make_async_copy(src, dst, local.at[4 + n])
        for n, (src, dst) in enumerate(
            (
                (blk_in, blk),
                (pao_size_in, pao_size),
                (cabs_size_in, cabs_size),
                (blk_in, blk_rows),
                (weight_in, weight),
            )
        )
    ]
    for copy in load:
        copy.start()
    greet(
        [place.along(a, s) for a in ("y", "z") for s in (1, -1)]
        + [place.partner(), place.beside(1), place.beside(-1)]
    )
    load[0].wait()
    cuts = ((0, 1024), (1024, 896))
    first = Gather(
        place,
        Wires(send_a, recv_a),
        lambda h: own.at[pl.ds(0, 48), pl.ds(1920 * h, 1920)],
        lambda h, atom: every.at[32 * h + atom],
        lambda h, atom, s: every.at[32 * h + atom, :, pl.ds(*cuts[s])],
        lambda h, k, m: m if h == 0 else k,
    )
    sums, gathers = [], [first]
    for r, (_, top, count) in enumerate(PARTS):
        sums.append(
            RingSum(
                place,
                Wires(send_b.at[r], recv_b, 3 * r),
                count,
                lambda k, span, r=r: parts[r].at[k, span],
                nears[r],
                finals[r],
            )
        )
        half = (count + 1) // 2
        span = ((top, half), (top + half, count - half))
        pieces = [
            ((t, (n + 1) // 2), (t + (n + 1) // 2, n // 2)) for t, n in span
        ]

        def tiles(atom, start, n):
            return held.at[pl.ds(atom * HELD + start, n)]

        gathers.append(
            Gather(
                place,
                Wires(send_c.at[r], recv_c, 31 * r),
                lambda h, span=span: tiles(place.me, *span[h]),
                lambda h, atom, span=span: tiles(atom, *span[h]),
                lambda h, atom, s, pieces=pieces: tiles(atom, *pieces[h][s]),
                lambda h, k, m: 0,
            )
        )

    def roots():
        w = weight[...].astype(jnp.float32)
        spot = lax.broadcasted_iota(jnp.int32, (8, 48), 1) - 12 * x
        row = lax.broadcasted_iota(jnp.int32, (8, 48), 0)

        def column(b, shift, mask):
            at = jnp.logical_and(mask, spot == row + shift)
            return jnp.where(at, jnp.broadcast_to(w[b : b + 1], (8, 48)), 0.0)

        return [
            jnp.sqrt(jnp.sum(part_w, axis=1, keepdims=True))
            for part_w in (
                column(0, 0, row >= 0),
                column(1, 0, row >= 0),
                column(0, 8, row < 4) + column(1, 4, row >= 4),
            )
        ]

    nt = (((1,), (1,)), ((), ()))

    def line_products(i):
        line = lax.rem(place.y + OFFSETS[i] + 4, 4)
        g = None
        for h in range(2):
            rows = every[pl.ds(32 * h + line * 8, 8)].reshape(384, 1920)
            d = lax.dot_general(
                own[48:, 1920 * h : 1920 * (h + 1)], rows, nt,
                preferred_element_type=jnp.float32,
            )
            g = d if g is None else g + d
        r = [i in lines for lines, _, _ in PARTS].index(True)
        start = 9 * PARTS[r][0].index(i)
        for c in range(3):
            col = g[:, 128 * c : 128 * c + 128]
            for k in range(4):
                a, b = 12 * k, 48 + 12 * k
                parts[r][k, start + c] = col[a : a + 8]
                parts[r][k, start + 3 + c] = col[b : b + 8]
                parts[r][k, start + 6 + c] = jnp.concatenate(
                    [col[a + 8 : a + 12], col[b + 8 : b + 12]], axis=0
                )

    def pick_blocks(i):
        line = lax.rem(place.y + OFFSETS[i] + 4, 4)
        slot = SLOTS[i]
        names = blk_rows[...]
        for j in range(4):
            odd = []
            for n in range(2):
                hit = jnp.where(names == 2 * (line * 8 + 2 * j + n) + 1, 1, 0)
                hit = jnp.max(jnp.max(hit, axis=1, keepdims=True), axis=0, keepdims=True)
                odd.append(jnp.broadcast_to(hit, (24, 1920)) > 0)
            for h in range(2):
                got = []
                for n in range(2):
                    rows = every[32 * h + line * 8 + 2 * j + n].astype(jnp.float32)
                    got.append(jnp.where(odd[n], rows[24:], rows[:24]))
                at = 192 * slot + 48 * j
                chosen[h, at : at + 48] = jnp.concatenate(got, axis=0).astype(jnp.bfloat16)

    def margin_block(a, b):
        g = None
        for h in range(2):
            d = lax.dot_general(
                chosen[h, 128 * a : 128 * a + 128], chosen[h, 256 * b : 256 * b + 256], nt,
                preferred_element_type=jnp.float32,
            )
            g = d if g is None else g + d
        for t in range(16):
            for c in range(2):
                margins[(16 * a + t) * 6 + 2 * b + c] = g[
                    8 * t : 8 * t + 8, 128 * c : 128 * c + 128
                ]

    mine = place.me * HELD

    def keep_part(r, root):
        total = sums[r].total()
        lines, top, count = PARTS[r]
        for n in range(3 * len(lines)):
            held[pl.ds(mine + top + 3 * n, 3)] = total[3 * n : 3 * n + 3] * root[n % 3]

    def line_sem(i):
        return ("d", 0, i)

    def needs(op):
        name, g = op[0], op[1]
        if name in (LINE, PICK):
            return [line_sem(g)]
        if name == BLOCK:
            return []
        if name in (FAR, PLAIN):
            return []
        if name == MIXED:
            return [("near", g, op[2])]
        if name == KEEP:
            return []
        h = op[2]
        reach = lambda k: [] if k == 0 else [("1", g, h, k - 1)] if k < 3 else [("1s", g, h)]
        if name == START:
            return []
        if name == RELAY:
            return [("1", g, h, op[3])]
        if name == SPREAD:
            return reach(op[3])
        if name == PASS:
            return [("2", g, h, op[3], op[4])]
        k, m = op[3], op[4]
        return reach(k) if m == 0 else [("2", g, h, k, m - 1)] if m < 3 else [("2s", g, h, k)]

    def settle(sem):
        kind, g = sem[0], sem[1]
        if kind == "d":
            first.from_partner(every.at[pl.ds(0, 8)], sem[2])
        elif kind == "near":
            sums[g].arrived(sem[2])
        else:
            at = {"1": "arrived1", "1s": "arrived1s", "2": "arrived2", "2s": "arrived2s"}[kind]
            getattr(gathers[g], at)(*sem[2:])

    settled, loading, root = set(), load[1:], None
    for op in ORDER:
        for sem in needs(op):
            if sem not in settled:
                settle(sem)
                settled.add(sem)
        name, g = op[0], op[1]
        if name in (LINE, PICK) and loading:
            for copy in loading:
                copy.wait()
            loading, root = [], roots()
        if name == LINE:
            line_products(g)
        elif name == PICK:
            pick_blocks(g)
        elif name == BLOCK:
            margin_block(g, op[2])
        elif name == KEEP:
            keep_part(g, root)
        elif name in (FAR, PLAIN, MIXED):
            ring = sums[g]
            {FAR: ring.far, PLAIN: ring.plain, MIXED: ring.mixed}[name](op[2])
        else:
            net = gathers[g]
            {
                START: net.start,
                RELAY: net.relay,
                SPREAD: net.spread,
                PASS: net.pass_on,
                ACROSS: net.across,
            }[name](*op[2:])
    for r, (_, _, count) in enumerate(PARTS):
        gathers[r + 1].from_partner(held.at[pl.ds(0, 16 * count)], 0)

    lanes = lax.broadcasted_iota(jnp.int32, (8, 128), 1)
    subs = lax.broadcasted_iota(jnp.int32, (8, 128), 0)

    def half_of(n, bits):
        return lax.shift_right_logical(n, jnp.int32(bits))

    def one_pair(p):
        picks = [blk[l, p] for l in range(4)]
        base = [half_of(b, 1) * HELD for b in picks]
        par = [jnp.bitwise_and(b, 1) for b in picks]
        lines = [half_of(b, 4) for b in picks]
        seats = []
        for b, line in zip(picks, lines):
            away = jnp.bitwise_and(line - place.y, 3)
            slot = jnp.bitwise_xor(away, half_of(away, 1))
            seats.append(slot * 8 + jnp.bitwise_and(half_of(b, 1), 7))
        acc = [None] * 20
        for l in range(4):
            off = jnp.bitwise_and(picks[l], 15) * 24
            u = half_of(off, 7)
            rem = jnp.bitwise_and(off, 127)
            turn = jnp.bitwise_and(24 * l + 128 - rem, 127)
            whole = lanes >= rem
            here = jnp.logical_and(lanes >= 24 * l, lanes < 24 * l + 24)
            off = seats[l] * 24
            um = half_of(off, 7)
            rem = jnp.bitwise_and(off, 127)
            turn_m = jnp.bitwise_and(24 * l + 128 - rem, 127)
            whole_m = lanes >= rem

            def place_in(n, two, whole, turn):
                moved = pltpu.roll(jnp.where(whole, two[0], two[1]), turn, 1)
                old = jnp.zeros_like(moved) if acc[n] is None else acc[n]
                acc[n] = jnp.where(here, moved, old)

            for k in range(4):
                m = margins[pl.ds(seats[k] * 18 + um, 14)]
                for t in range(3):
                    place_in(3 * k + t, (m[6 * t], m[6 * t + 1]), whole_m, turn_m)
                away = jnp.bitwise_and(lines[l] - lines[k], 3)
                at = base[k] + jnp.bitwise_xor(away, half_of(away, 1)) * 9 + u
                c = held[pl.ds(at + par[k] * 3, 2)]
                place_in(12 + 2 * k, (c[0], c[1]), whole, turn)
                c = held[pl.ds(at + 6, 2)]
                place_in(13 + 2 * k, (c[0], c[1]), whole, turn)
        limit = cabs_size[p] - 12 * x
        for k in range(4):
            first = subs < limit - 48 * k
            low = 4 * par[k]
            second = jnp.logical_and(
                jnp.logical_and(subs >= low, subs < low + 4),
                subs < limit - 48 * k - 8 + low,
            )
            acc[12 + 2 * k] = jnp.where(first, acc[12 + 2 * k], 0.0)
            acc[13 + 2 * k] = jnp.where(second, acc[13 + 2 * k], 0.0)
        margin = jnp.concatenate(acc[:12], axis=0)
        c = jnp.concatenate(acc[12:], axis=0)
        hi = c.astype(jnp.bfloat16)
        lo = (c - hi.astype(jnp.float32)).astype(jnp.bfloat16)
        prod = lax.dot_general(
            jnp.concatenate([hi, lo, hi], axis=0),
            jnp.concatenate([hi, hi, lo], axis=0),
            (((0,), (0,)), ((), ())),
            preferred_element_type=jnp.float32,
        )
        return margin - prod[:96]

    left, right = place.beside(-1), place.beside(1)
    klass = sums[0].klass

    def copy_v(kind, q):
        e, o = 2 * q, 2 * q + 1
        src, dst, device, at = (
            lambda: (vals.at[klass(2) * 16 + e], vnear.at[2 * q], left, 3 * q),
            lambda: (vals.at[klass(2) * 16 + o], vnear.at[2 * q + 1], right, 3 * q + 1),
            lambda: (vals.at[klass(-1) * 16 + o], vfinal.at[o], left, 3 * q + 2),
            lambda: (vals.at[klass(1) * 16 + e], vfinal.at[16 + e], right, 3 * q + 2),
            lambda: (vals.at[klass(-1) * 16 + e], vfinal.at[e], left, 3 * q + 2),
            lambda: (vals.at[klass(1) * 16 + o], vfinal.at[16 + o], right, 3 * q + 2),
        )[kind]()
        return Wires(send_v, recv_v).copy(src, dst, at, device)

    def second_step(q):
        e, o = klass(-1) * 16 + 2 * q, klass(1) * 16 + 2 * q + 1
        copy_v(0, q).wait_recv()
        vals[e] = vals[e] + vnear[2 * q]
        copy_v(4, q).start()
        copy_v(1, q).wait_recv()
        vals[o] = vals[o] + vnear[2 * q + 1]
        copy_v(5, q).start()

    wide = lax.broadcasted_iota(jnp.int32, (96, 128), 1)

    def group(g):
        v = [one_pair(g * 4 + n) for n in range(4)]
        r1 = pltpu.roll(v[1], 96, 1)
        r2 = pltpu.roll(v[2], 64, 1)
        r3 = pltpu.roll(v[3], 32, 1)
        packed = (
            jnp.where(wide < 96, v[0], r1),
            jnp.where(wide < 64, r1, r2),
            jnp.where(wide < 32, r2, r3),
        )
        for c in range(3):
            for k in range(4):
                vals[k * 16 + g, :, 128 * c : 128 * c + 128] = packed[c][24 * k : 24 * k + 24]

    @pl.loop(0, 8)
    def _(q):
        group(2 * q)
        copy_v(0, q).start()
        copy_v(3, q).start()
        group(2 * q + 1)
        copy_v(1, q).start()
        copy_v(2, q).start()

        @pl.when(q >= 3)
        def _():
            second_step(q - 3)

    for q in range(8 - 3, 8):
        second_step(q)

    narrow = lax.broadcasted_iota(jnp.int32, (24, 128), 1)
    deep = lax.broadcasted_iota(jnp.int32, (24, 128), 0) + 24 * x

    @pl.loop(0, 8)
    def _(q):
        view = vfinal.at[pl.ds(0, 4)]
        Wires(send_v, recv_v).wait(view, 3 * q + 2, left)
        for half in range(2):
            g = 2 * q + half
            t = vals[x * 16 + g] + (vfinal[g] + vfinal[16 + g])
            t0, t1, t2 = t[:, :128], t[:, 128:256], t[:, 256:]
            v = (
                t0,
                jnp.where(narrow < 32, pltpu.roll(t0, 32, 1), pltpu.roll(t1, 32, 1)),
                jnp.where(narrow < 64, pltpu.roll(t1, 64, 1), pltpu.roll(t2, 64, 1)),
                pltpu.roll(t2, 96, 1),
            )
            for n in range(4):
                size = pao_size[g * 4 + n]
                keep = jnp.logical_and(deep < size, narrow < size)
                out[g * 4 + n] = jnp.where(keep, v[n], 0.0)[:, :96]

    first.wires.drain(every.at[pl.ds(0, 62)], left)
    for r, (_, _, count) in enumerate(PARTS):
        sums[r].wires.drain(held.at[pl.ds(0, 3 * count)], left)
        gathers[r + 1].wires.drain(held.at[pl.ds(0, 31 * count)], left)
    Wires(send_v, recv_v).drain(vals.at[pl.ds(0, 48)], left)


def fused(blk, pao_size, cabs_size, pao, cabs, weight):
    dma = pltpu.SemaphoreType.DMA
    vmem = pl.BlockSpec(memory_space=pltpu.VMEM)
    hbm = pl.BlockSpec(memory_space=pltpu.HBM)
    f32 = jnp.float32
    return pl.pallas_call(
        kernel,
        out_shape=jax.ShapeDtypeStruct((64, 24, 96), f32),
        in_specs=[hbm] * 6,
        out_specs=vmem,
        scratch_shapes=[
            pltpu.SMEM((4, 64), jnp.int32),
            pltpu.SMEM((64,), jnp.int32),
            pltpu.SMEM((64,), jnp.int32),
            pltpu.VMEM((4, 64), jnp.int32),
            pltpu.VMEM((2, 48), jnp.bfloat16),
            pltpu.VMEM((144, 3840), jnp.bfloat16),
            pltpu.VMEM((64, 48, 1920), jnp.bfloat16),
            pltpu.VMEM((2, 768, 1920), jnp.bfloat16),
            pltpu.VMEM((CHOSEN, 8, 128), f32),
            [pltpu.VMEM((4, n, 8, 128), f32) for _, _, n in PARTS],
            [pltpu.VMEM((2, (n + 1) // 2, 8, 128), f32) for _, _, n in PARTS],
            [pltpu.VMEM((2, n, 8, 128), f32) for _, _, n in PARTS],
            pltpu.VMEM((32 * HELD, 8, 128), f32),
            pltpu.VMEM((64, 24, 384), f32),
            pltpu.VMEM((16, 24, 384), f32),
            pltpu.VMEM((32, 24, 384), f32),
            dma,
            dma((Gather.TOTAL + 4,)),
            dma((len(PARTS),)),
            dma((3 * len(PARTS),)),
            dma((len(PARTS),)),
            dma((31 * len(PARTS),)),
            dma,
            dma((24,)),
            dma((9,)),
        ],
        compiler_params=pltpu.CompilerParams(
            collective_id=0, has_side_effects=True, vmem_limit_bytes=56 * 1024 * 1024
        ),
        name="fused",
    )(blk, pao_size, cabs_size, pao, cabs, weight)


def shards(pao_blocks, cabs_blocks, cabs_weight, pair_blocks, pao_size, cabs_size):
    return fused(
        pair_blocks.T,
        pao_size,
        cabs_size,
        pao_blocks.reshape(48, -1),
        cabs_blocks.reshape(96, -1),
        cabs_weight,
    )


def solution(mesh):
    placed = (
        P("atom", None, "aux"),
        P("atom", None, "aux"),
        P("atom", None),
        P("atom", None),
        P("atom"),
        P("atom"),
    )
    return jax.shard_map(
        shards, mesh=mesh, in_specs=placed, out_specs=P("atom", "aux", None), check_vma=False
    )
```

time: 101 us -> 94.3 us (0.934); the launches traced: 99.6 us -> 94 us
  Pallas kernels: 97.6 us -> 91.9 us
    pallas_call x1, Pallas kernels: 97.6 us -> 91.9 us  [fused(): pl.pallas_call(kernel, out_shape=jax.ShapeDtypeStruct((64, 24, 96), f32),...]
where the time goes in v5:
time: 94.3 us; the launch traced here: 94 us
  Pallas kernels  91.9 us (97%)
  local copies, waits for them, and re-layouts  2.06 us (2%)
    pallas_call x1, Pallas kernels, fused(): pl.pallas_call(kernel, out_shape=jax.ShapeDtypeStruct((64, 24, 96), f32),...  91.9 us
    unnamed x1, local copies, waits for them, and re-layouts  2.06 us

profile of v5, /device:TPU:1, one launch (start us, length us, event | category | flops | bytes accessed | tf_op | source)
XLA Modules:
  0.0 94.0 jit_solution(10467208501372808232)
XLA Ops:
  0.0 91.9 %fused.1 = f32[64,24,96]{2,1,0:T(8,128)} custom-call(s32[4,64]{1,0:T(4,128)} %bitcast.5, s32[64]{0:T(128)} %pao_size_in.1, s32[64]{0:T(128)} %cabs_size_in.1, bf16[48,3840]{1,0:T(8,128)(2,1)} %bitcast.4, bf16[96,3840]{1,0:T(8,128)(2,1)} %bitcast.3, bf16[2,48]{1,0:T(2,128)(2,1)} %weight_in.1), custom_call_target="tpu_custom_call" | custom-call | tf_op jit(solution)/shard_map/fused/pallas_call | solution.py:660
  91.9 2.1 %copy.8 = f32[64,24,96]{2,1,0:T(8,128)} copy(f32[64,24,96]{2,1,0:T(8,128)} %fused.1) | data formatting | bytes 1179648

commit v6 on v5

--- a/solution.py
+++ b/solution.py
@@ -616,11 +616,11 @@
         copy_v(1, q).start()
         copy_v(2, q).start()
 
-        @pl.when(q >= 3)
+        @pl.when(q >= 4)
         def _():
-            second_step(q - 3)
-
-    for q in range(8 - 3, 8):
+            second_step(q - 4)
+
+    for q in range(4, 8):
         second_step(q)
 
     narrow = lax.broadcasted_iota(jnp.int32, (24, 128), 1)

time: 94.3 us -> 94.2 us (level)
  no operation moved by 1% of the time
where the time goes in v6:
time: 94.2 us; the launch traced here: 94.1 us
  Pallas kernels  92 us (98%)
  local copies, waits for them, and re-layouts  2.06 us (2%)
    pallas_call x1, Pallas kernels, fused(): pl.pallas_call(kernel, out_shape=jax.ShapeDtypeStruct((64, 24, 96), f32),...  92 us
    unnamed x1, local copies, waits for them, and re-layouts  2.06 us

profile of v6, /device:TPU:1, one launch (start us, length us, event | category | flops | bytes accessed | tf_op | source)
XLA Modules:
  0.0 94.1 jit_solution(15973458247032979359)
XLA Ops:
  0.0 92.0 %fused.1 = f32[64,24,96]{2,1,0:T(8,128)} custom-call(s32[4,64]{1,0:T(4,128)} %bitcast.5, s32[64]{0:T(128)} %pao_size_in.1, s32[64]{0:T(128)} %cabs_size_in.1, bf16[48,3840]{1,0:T(8,128)(2,1)} %bitcast.4, bf16[96,3840]{1,0:T(8,128)(2,1)} %bitcast.3, bf16[2,48]{1,0:T(2,128)(2,1)} %weight_in.1), custom_call_target="tpu_custom_call" | custom-call | tf_op jit(solution)/shard_map/fused/pallas_call | solution.py:660
  92.0 2.1 %copy.8 = f32[64,24,96]{2,1,0:T(8,128)} copy(f32[64,24,96]{2,1,0:T(8,128)} %fused.1) | data formatting | bytes 1179648
